TPU v7x, 32 devices: a whole 2x2x4 slice. The times are simulated.
32 devices in a mesh: rows: 8 (over z, x), ka: 4 (over y, core).
Axes of the slice: x: 2, y: 2, z: 4, core: 2. Of those that a mesh axis runs over, the one named last changes fastest.
Arguments:
- pair_repr: bfloat16 [512, 512, 128], P('rows', 'ka'), may hold values from -6 to 6
- pair_mask: int32 [512, 512], P('rows', 'ka'), may hold values 0 or 1
- ln_gain: float32 [128], replicated, may hold values from 0.1 to 1.9
- ln_bias: float32 [128], replicated, may hold values from -3 to 3
- w_proj: bfloat16 [128, 256], replicated, may hold values from -0.5 to 0.5
- w_gate: bfloat16 [128, 256], replicated, may hold values from -0.5 to 0.5
- w_out_gate: bfloat16 [128, 128], replicated, may hold values from -0.5 to 0.5
- out_gain: float32 [128], replicated, may hold values from 0.1 to 1.9
- out_bias: float32 [128], replicated, may hold values from -3 to 3
- w_out: bfloat16 [128, 128], replicated, may hold values from -0.5 to 0.5
Outputs:
- update: bfloat16 [512, 512, 128], P('rows', 'ka')
All inputs are finite; a program needn't handle non-finite values. No bound on the sum of `pair_mask` on one device may be relied on, other than what follows from the above.
Results may differ from a plain program's by a relative error of at most 0.015.
Values may be sent and summed in bfloat16 or wider, within the bound.
A program may use at most 64 MiB of HBM per device.

v0:
```python
import functools

import jax
import jax.numpy as jnp
from jax import lax
from jax.experimental import pallas as pl
from jax.experimental.pallas import tpu as pltpu
from jax.sharding import PartitionSpec as P

MESH = pl.DeviceIdType.MESH
CHUNK = 16
PITCH = 24


def layer_norm(values, gain_vec, bias_vec):
    center = jnp.mean(values, axis=-1, keepdims=True)
    deviate = values - center
    spread = jnp.mean(deviate * deviate, axis=-1, keepdims=True)
    return deviate * lax.rsqrt(spread + 1e-05) * gain_vec + bias_vec


def sigmoid(logits):
    return 0.5 + 0.5 * jnp.tanh(0.5 * logits)


def kernel(
    rows_n, ka_n, halves, groups,
    pair_hbm, mask_ref, ln_gain_ref, ln_bias_ref, w_proj_ref, w_gate_ref, w_out_gate_ref,
    out_gain_ref, out_bias_ref, w_out_ref,
    out_hbm,
    pair_ref, out_ref, edges, wide, normed, gates, left, right, tri, back, w_cat, gain_col, bias_col,
    load_sem, store_sem, recv_left, recv_right, send_left, send_right, recv_tri, send_tri,
):
    row = lax.axis_index("rows")
    col = lax.axis_index("ka")
    row_count, col_count, chans = pair_ref.shape
    hidden = w_out_ref.shape[0]
    group_rows = rows_n // halves
    members = group_rows * ka_n
    share = hidden // members
    half = row // group_rows
    spot = row % group_rows
    member = spot * ka_n + col
    chunks = row_count // CHUNK

    sub = share // groups
    planes = wide.reshape(2 * hidden, PITCH, col_count)

    def chunk_rows(chunk):
        return pl.ds(pl.multiple_of(chunk * CHUNK, CHUNK), CHUNK)

    def load(chunk):
        rows = chunk_rows(chunk)
        return pltpu.make_async_copy(pair_hbm.at[rows], pair_ref.at[rows], load_sem.at[chunk])

    for chunk in range(chunks):
        load(chunk).start()

    barrier = pltpu.get_barrier_semaphore()

    def greet(step, carry):
        to_row = (row + step // ka_n) % rows_n
        to_col = (col + step % ka_n) % ka_n
        pl.semaphore_signal(barrier, inc=1, device_id=(to_row, to_col), device_id_type=MESH)
        return carry

    lax.fori_loop(1, rows_n * ka_n, greet, 0)

    def turned(ref):
        return ref[...].astype(jnp.float32).T.astype(jnp.bfloat16)

    w_cat[: 2 * hidden, :] = turned(w_gate_ref)
    w_cat[2 * hidden :, :] = turned(w_proj_ref)

    own_cols = pl.ds(pl.multiple_of(col * col_count, 128), col_count)

    def left_copy(group, first, size, to_spot, to_col):
        to_member = to_spot * ka_n + to_col
        return pltpu.make_async_remote_copy(
            src_ref=edges.at[pl.ds(to_member * share + group * sub, sub), pl.ds(first, size), :],
            dst_ref=left.at[pl.ds(group * sub, sub), pl.ds(spot * row_count + first, size), own_cols],
            send_sem=send_left,
            recv_sem=recv_left.at[group],
            device_id=(half * group_rows + to_spot, to_col),
            device_id_type=MESH,
        )

    def right_copy(group, first, size, turn, to_spot, to_col):
        to_member = to_spot * ka_n + to_col
        to_half = (half + turn) % halves
        return pltpu.make_async_remote_copy(
            src_ref=edges.at[
                pl.ds(hidden + to_member * share + group * sub, sub), pl.ds(first, size), :
            ],
            dst_ref=right.at[pl.ds(group * sub, sub), pl.ds(row * row_count + first, size), own_cols],
            send_sem=send_right.at[turn],
            recv_sem=recv_right.at[group],
            device_id=(to_half * group_rows + to_spot, to_col),
            device_id_type=MESH,
        )

    def partner(step):
        return (spot + step % group_rows) % group_rows, (col + step // group_rows) % ka_n

    def make_chunk(chunk):
        load(chunk).wait()

        def one_row(local, carry):
            at = chunk * CHUNK + local
            values = pair_ref[at].astype(jnp.float32)
            plain = layer_norm(values, ln_gain_ref[...], ln_bias_ref[...]).astype(jnp.bfloat16)
            normed[at] = plain
            both = lax.dot_general(
                w_cat[...], plain, (((1,), (1,)), ((), ())), preferred_element_type=jnp.float32
            )
            mask_row = mask_ref[pl.ds(at, 1), :].astype(jnp.float32)
            made = sigmoid(both[: 2 * hidden]) * both[2 * hidden :] * mask_row
            wide[pl.ds(local, 2 * hidden, stride=PITCH), :] = made
            return carry

        lax.fori_loop(0, CHUNK, one_row, 0, unroll=2)
        edges[:, chunk_rows(chunk), :] = planes[:, :CHUNK, :].astype(jnp.bfloat16)

    def send_part(group, first, size):
        def near(step, carry):
            to_spot, to_col = partner(step)
            left_copy(group, first, size, to_spot, to_col).start()
            right_copy(group, first, size, 0, to_spot, to_col).start()
            return carry

        lax.fori_loop(1, members, near, 0)

        def far(step, carry):
            for turn in range(1, halves):
                right_copy(group, first, size, turn, *partner(step)).start()
            return carry

        lax.fori_loop(0, members, far, 0)

    def send_chunk(chunk):
        send_part(0, pl.multiple_of(chunk * CHUNK, CHUNK), CHUNK)

    make_chunk(0)
    pl.semaphore_wait(barrier, rows_n * ka_n - 1)
    send_chunk(0)

    def rest(chunk, carry):
        make_chunk(chunk)
        send_chunk(chunk)
        return carry

    lax.fori_loop(1, chunks, rest, 0)

    for group in range(1, groups):
        send_part(group, 0, row_count)

    for group in range(groups):
        mine = pl.ds(group * sub, sub)
        pltpu.make_async_copy(
            edges.at[pl.ds(member * share + group * sub, sub)],
            left.at[mine, pl.ds(spot * row_count, row_count), own_cols],
            recv_left.at[group],
        ).start()
        pltpu.make_async_copy(
            edges.at[pl.ds(hidden + member * share + group * sub, sub)],
            right.at[mine, pl.ds(row * row_count, row_count), own_cols],
            recv_right.at[group],
        ).start()

    gain_col[...] = jnp.broadcast_to(out_gain_ref[...], (col_count, hidden)).T
    bias_col[...] = jnp.broadcast_to(out_bias_ref[...], (col_count, hidden)).T

    def gate_row(at, carry):
        gates[at] = sigmoid(
            jnp.dot(normed[at], w_out_gate_ref[...], preferred_element_type=jnp.float32)
        )
        return carry

    lax.fori_loop(0, row_count, gate_row, 0, unroll=2)

    def one_channel(chan, carry):
        tri[chan] = lax.dot_general(
            left[chan], right[chan], (((1,), (1,)), ((), ())), preferred_element_type=jnp.float32
        ).astype(jnp.bfloat16)
        return carry

    def tri_part(group, chunk, to_spot, to_col):
        return tri.at[
            pl.ds(group * sub, sub),
            pl.ds(to_spot * row_count + chunk * CHUNK, CHUNK),
            pl.ds(pl.multiple_of(to_col * col_count, 128), col_count),
        ]

    for group in range(groups):
        mine = pl.ds(group * sub, sub)
        pltpu.make_async_copy(left.at[mine], left.at[mine], recv_left.at[group]).wait()
        pltpu.make_async_copy(right.at[mine], right.at[mine], recv_right.at[group]).wait()
        lax.fori_loop(group * sub, (group + 1) * sub, one_channel, 0)

        def give_chunk(chunk, carry):
            slot = back.at[pl.ds(member * share + group * sub, sub), chunk_rows(chunk), :]

            def give(step, inner):
                to_spot, to_col = partner(step)
                pltpu.make_async_remote_copy(
                    src_ref=tri_part(group, chunk, to_spot, to_col),
                    dst_ref=slot,
                    send_sem=send_tri,
                    recv_sem=recv_tri.at[chunk],
                    device_id=(half * group_rows + to_spot, to_col),
                    device_id_type=MESH,
                ).start()
                return inner

            lax.fori_loop(1, members, give, 0)
            pltpu.make_async_copy(
                tri_part(group, chunk, spot, col), slot, recv_tri.at[chunk]
            ).start()
            return carry

        lax.fori_loop(0, chunks, give_chunk, 0)

    def finish(chunk, carry):
        first = pl.multiple_of(chunk * CHUNK, CHUNK)
        arrived = back.at[:, chunk_rows(chunk), :]
        pltpu.make_async_copy(arrived, arrived, recv_tri.at[chunk]).wait()
        sums = back[:, pl.ds(first, CHUNK), :].astype(jnp.float32)
        center = jnp.mean(sums, axis=0, keepdims=True)
        deviate = sums - center
        spread = jnp.mean(deviate * deviate, axis=0, keepdims=True)
        scaled = deviate * lax.rsqrt(spread + 1e-05)
        planes[:hidden, :CHUNK, :] = scaled

        def one_row(local, inner):
            at = first + local
            chans_first = wide[pl.ds(local, hidden, stride=PITCH), :]
            tri_normed = (chans_first * gain_col[...] + bias_col[...]).astype(jnp.bfloat16)
            projected = lax.dot_general(
                tri_normed, w_out_ref[...], (((0,), (0,)), ((), ())), preferred_element_type=jnp.float32
            )
            out_ref[at] = (gates[at] * projected).astype(jnp.bfloat16)
            return inner

        lax.fori_loop(0, CHUNK, one_row, 0, unroll=2)
        pltpu.make_async_copy(
            out_ref.at[chunk_rows(chunk)], out_hbm.at[chunk_rows(chunk)], store_sem
        ).start()
        return carry

    lax.fori_loop(0, chunks, finish, 0)
    pltpu.make_async_copy(out_ref, out_hbm, store_sem).wait()

    others = pl.ds(0, (members - 1) * share)
    pltpu.make_async_copy(edges.at[others], edges.at[others], send_left).wait()
    pltpu.make_async_copy(edges.at[others], edges.at[others], send_right.at[0]).wait()
    for turn in range(1, halves):
        every = pl.ds(0, hidden)
        pltpu.make_async_copy(edges.at[every], edges.at[every], send_right.at[turn]).wait()
    pltpu.make_async_copy(back.at[others], back.at[others], send_tri).wait()


def fused(rows_n, ka_n, halves, args):
    pair_repr, pair_mask, ln_gain, ln_bias, w_proj, w_gate, w_out_gate, out_gain, out_bias, w_out = args
    row_count, col_count, chans = pair_repr.shape
    hidden = w_out.shape[0]
    members = rows_n // halves * ka_n
    share = hidden // members
    groups = 2 if share % 2 == 0 else 1
    half = jnp.bfloat16
    return pl.pallas_call(
        functools.partial(kernel, rows_n, ka_n, halves, groups),
        out_shape=jax.ShapeDtypeStruct(pair_repr.shape, half),
        in_specs=[pl.BlockSpec(memory_space=pl.ANY)] + [pl.BlockSpec(memory_space=pltpu.VMEM)] * 9,
        out_specs=pl.BlockSpec(memory_space=pl.ANY),
        scratch_shapes=[
            pltpu.VMEM((row_count, col_count, chans), half),
            pltpu.VMEM((row_count, col_count, chans), half),
            pltpu.VMEM((2 * hidden, row_count, col_count), half),
            pltpu.VMEM((2 * hidden * PITCH, col_count), jnp.float32),
            pltpu.VMEM((row_count, col_count, chans), half),
            pltpu.VMEM((row_count, col_count, chans), jnp.float32),
            pltpu.VMEM((share, rows_n // halves * row_count, ka_n * col_count), half),
            pltpu.VMEM((share, rows_n * row_count, ka_n * col_count), half),
            pltpu.VMEM((share, rows_n // halves * row_count, ka_n * col_count), half),
            pltpu.VMEM((hidden, row_count, col_count), half),
            pltpu.VMEM((4 * hidden, chans), half),
            pltpu.VMEM((hidden, col_count), jnp.float32),
            pltpu.VMEM((hidden, col_count), jnp.float32),
            pltpu.SemaphoreType.DMA((row_count // CHUNK,)),
            pltpu.SemaphoreType.DMA,
            pltpu.SemaphoreType.DMA((groups,)),
            pltpu.SemaphoreType.DMA((groups,)),
            pltpu.SemaphoreType.DMA,
            pltpu.SemaphoreType.DMA((halves,)),
            pltpu.SemaphoreType.DMA((row_count // CHUNK,)),
            pltpu.SemaphoreType.DMA,
        ],
        compiler_params=pltpu.CompilerParams(
            collective_id=0, has_side_effects=True, vmem_limit_bytes=60 * 2**20
        ),
    )(
        pair_repr, pair_mask, ln_gain[None], ln_bias[None], w_proj, w_gate, w_out_gate,
        out_gain[None], out_bias[None], w_out,
    )


def plain(args):
    pair_repr, pair_mask, ln_gain, ln_bias, w_proj, w_gate, w_out_gate, out_gain, out_bias, w_out = args
    row_count, col_count, chans = pair_repr.shape
    hidden = w_out.shape[0]
    normed = layer_norm(pair_repr.astype(jnp.float32), ln_gain, ln_bias).astype(jnp.bfloat16)
    flat_rows = normed.reshape(row_count * col_count, chans)
    projected = jnp.dot(flat_rows, w_proj, preferred_element_type=jnp.float32)
    gate_logits = jnp.dot(flat_rows, w_gate, preferred_element_type=jnp.float32)
    mask_col = pair_mask.reshape(row_count * col_count, 1).astype(jnp.float32)
    edges = (jax.nn.sigmoid(gate_logits) * projected * mask_col).astype(jnp.bfloat16)
    edges = edges.reshape(row_count, col_count, 2 * hidden)
    partial_sums = jnp.einsum(
        "ikh,jkh->ijh",
        edges[:, :, :hidden],
        lax.all_gather(edges[:, :, hidden:], "rows", axis=0, tiled=True),
        preferred_element_type=jnp.float32,
    )
    triangle = lax.psum_scatter(
        partial_sums.astype(jnp.bfloat16), "ka", scatter_dimension=1, tiled=True
    ).astype(jnp.float32)
    tri_normed = layer_norm(triangle, out_gain, out_bias).astype(jnp.bfloat16)
    out_gate = jax.nn.sigmoid(jnp.dot(flat_rows, w_out_gate, preferred_element_type=jnp.float32))
    projected_out = jnp.dot(
        tri_normed.reshape(row_count * col_count, hidden), w_out, preferred_element_type=jnp.float32
    )
    return (out_gate * projected_out).astype(jnp.bfloat16).reshape(row_count, col_count, chans)


def body(rows_n, ka_n, *args):
    row_count, col_count, chans = args[0].shape
    hidden = args[-1].shape[0]
    halves = 2 if rows_n % 2 == 0 else 1
    members = rows_n // halves * ka_n
    aligned = row_count % CHUNK == 0 and col_count % 128 == 0 and chans % 128 == 0 and hidden % 128 == 0
    if aligned and hidden % members == 0 and col_count == hidden:
        return fused(rows_n, ka_n, halves, args)
    return plain(args)


def solution(mesh):
    placed = (P("rows", "ka", None), P("rows", "ka"), P(), P(), P(), P(), P(), P(), P(), P())
    return jax.shard_map(
        functools.partial(body, mesh.shape["rows"], mesh.shape["ka"]),
        mesh=mesh, in_specs=placed, out_specs=P("rows", "ka", None), check_vma=False,
    )
```

profile of v0, /device:TPU:0, one launch (start us, length us, event | category | flops | bytes accessed | tf_op | source)
XLA Modules:
  0.0 129.6 jit_solution(222926772038774210)
XLA Ops:
  0.0 126.5 %shard_map.100 = bf16[64,128,128]{2,1,0:T(8,128)(2,1)} custom-call(bf16[64,128,128]{2,1,0:T(8,128)(2,1)} %pair_hbm.1, s32[64,128]{1,0:T(8,128)} %mask_ref.1, f32[1,128]{1,0:T(1,128)} %bitcast.4, f32[1,128]{1,0:T(1,128)} %bitcast.5, bf16[128,256]{1,0:T(8,128)(2,1)} %w_proj_ref.1, bf16[128,256]{1,0:T(8,128)(2,1)} %w_gate_ref.1, ...), custom_call_target="tpu_custom_call" | custom-call | tf_op jit(solution)/shard_map/pallas_call | solution.py:270
  126.5 3.2 %copy.12 = bf16[64,128,128]{2,1,0:T(8,128)(2,1)} copy(bf16[64,128,128]{2,1,0:T(8,128)(2,1)} %shard_map.100) | data formatting | bytes 4194304
where the time goes:
time: 132 us; the launch traced here: 130 us
  Pallas kernels  126 us (95%)
  local copies, waits for them, and re-layouts  3.16 us (2%)
    pallas_call x1, Pallas kernels, fused(): pl.pallas_call(functools.partial(kernel, rows_n, ka_n, halves, groups), o...  126 us
    unnamed x1, local copies, waits for them, and re-layouts  3.16 us

commit v1 on v0

v1 whole, which is shorter than its diff:
```python
import functools

import jax
import jax.numpy as jnp
from jax import lax
from jax.experimental import pallas as pl
from jax.experimental.pallas import tpu as pltpu
from jax.sharding import PartitionSpec as P

MESH = pl.DeviceIdType.MESH
CHUNK = 16
PITCH = 24
EARLY = 2
MAKE_UNROLL = 8
GATE_UNROLL = 8
FINISH_UNROLL = 16


def layer_norm(values, gain_vec, bias_vec):
    center = jnp.mean(values, axis=-1, keepdims=True)
    deviate = values - center
    spread = jnp.mean(deviate * deviate, axis=-1, keepdims=True)
    return deviate * lax.rsqrt(spread + 1e-05) * gain_vec + bias_vec


def sigmoid(logits):
    return 0.5 + 0.5 * jnp.tanh(0.5 * logits)


def kernel(
    rows_n, ka_n, early,
    pair_hbm, mask_ref, ln_gain_ref, ln_bias_ref, w_proj_ref, w_gate_ref, w_out_gate_ref,
    out_gain_ref, out_bias_ref, w_out_ref,
    out_hbm,
    pair_ref, out_ref, edges, wide, normed, gates, left, right, tri, back, w_cat, gain_col, bias_col,
    load_sem, store_sem, recv_left, recv_early, recv_right, recv_far, recv_tri,
    send_left, send_right, send_far, send_tri,
):
    row = lax.axis_index("rows")
    col = lax.axis_index("ka")
    row_count, col_count, chans = pair_ref.shape
    hidden = w_out_ref.shape[0]
    zone = rows_n // 4
    group_rows = 2 * zone
    members = group_rows * ka_n
    hubs = zone * ka_n
    share = hidden // hubs
    late = share - early
    chunks = row_count // CHUNK

    quarter = row // zone
    lane = row % zone
    half = quarter // 2
    spot = row % group_rows
    hub_q = 1 + half
    far_q = 2 - half
    edge_q = 3 * half
    place = half * (quarter - 2) + (1 - half) * (1 - quarter)
    inner = place == 0
    member = lane * ka_n + col
    planes = wide.reshape(2 * hidden, PITCH, col_count)

    def chunk_rows(chunk):
        return pl.ds(pl.multiple_of(chunk * CHUNK, CHUNK), CHUNK)

    def load(chunk):
        rows = chunk_rows(chunk)
        return pltpu.make_async_copy(pair_hbm.at[rows], pair_ref.at[rows], load_sem.at[chunk])

    for chunk in range(chunks):
        load(chunk).start()

    barrier = pltpu.get_barrier_semaphore()

    def greet(step, carry):
        to_row = (row + step // ka_n) % rows_n
        to_col = (col + step % ka_n) % ka_n
        pl.semaphore_signal(barrier, inc=1, device_id=(to_row, to_col), device_id_type=MESH)
        return carry

    lax.fori_loop(1, rows_n * ka_n, greet, 0)

    def turned(ref):
        return ref[...].astype(jnp.float32).T.astype(jnp.bfloat16)

    w_cat[: 2 * hidden, :] = turned(w_gate_ref)
    w_cat[2 * hidden :, :] = turned(w_proj_ref)

    own_cols = pl.ds(pl.multiple_of(col * col_count, 128), col_count)

    def left_ends(chan, count, first, size, to_member):
        return (
            edges.at[pl.ds(to_member * share + chan, count), pl.ds(first, size), :],
            left.at[pl.ds(chan, count), pl.ds(spot * row_count + first, size), own_cols],
        )

    def right_ends(chan, count, first, size, to_member):
        return (
            edges.at[pl.ds(hidden + to_member * share + chan, count), pl.ds(first, size), :],
            right.at[pl.ds(chan, count), pl.ds(row * row_count + first, size), own_cols],
        )

    def send_edges(ends, chan, count, first, size, sent, landed):
        def start(to_lane, to_col):
            here, there = ends(chan, count, first, size, to_lane * ka_n + to_col)
            pltpu.make_async_remote_copy(
                src_ref=here, dst_ref=there, send_sem=sent, recv_sem=landed,
                device_id=(quarter * zone + to_lane, to_col), device_id_type=MESH,
            ).start()

        def other(step, carry):
            start((lane + step % zone) % zone, (col + step // zone) % ka_n)
            return carry

        lax.fori_loop(1, hubs, other, 0)
        here, there = ends(chan, count, first, size, member)
        pltpu.make_async_copy(here, there, landed).start()

    def make_chunk(chunk):
        load(chunk).wait()

        def one_row(local, carry):
            at = chunk * CHUNK + local
            values = pair_ref[at].astype(jnp.float32)
            plain = layer_norm(values, ln_gain_ref[...], ln_bias_ref[...]).astype(jnp.bfloat16)
            normed[at] = plain
            both = lax.dot_general(
                w_cat[...], plain, (((1,), (1,)), ((), ())), preferred_element_type=jnp.float32
            )
            mask_row = mask_ref[pl.ds(at, 1), :].astype(jnp.float32)
            made = sigmoid(both[: 2 * hidden]) * both[2 * hidden :] * mask_row
            wide[pl.ds(local, 2 * hidden, stride=PITCH), :] = made
            return carry

        lax.fori_loop(0, CHUNK, one_row, 0, unroll=MAKE_UNROLL)
        edges[:, chunk_rows(chunk), :] = planes[:, :CHUNK, :].astype(jnp.bfloat16)

    def send_early(chunk):
        first = pl.multiple_of(chunk * CHUNK, CHUNK)
        send_edges(right_ends, 0, early, first, CHUNK, send_right, recv_early.at[0, chunk])
        send_edges(left_ends, 0, early, first, CHUNK, send_left, recv_left.at[0, 0])

    def send_late(group, carry):
        chan = early + group
        send_edges(right_ends, chan, 1, 0, row_count, send_right, recv_right.at[0, group])
        send_edges(left_ends, chan, 1, 0, row_count, send_left, recv_left.at[0, 1 + group])
        return carry

    def await_part(part, landed):
        pltpu.make_async_copy(part, part, landed).wait()

    def pass_on(part, to_q, landed):
        pltpu.make_async_remote_copy(
            src_ref=part, dst_ref=part, send_sem=send_far, recv_sem=landed,
            device_id=(to_q * zone + lane, col), device_id_type=MESH,
        ).start()

    def right_rows(chan, count, first, size):
        return right.at[pl.ds(chan, count), pl.ds(pl.multiple_of(first, CHUNK), size), :]

    def left_rows(chan, count, from_q):
        first = pl.multiple_of(from_q % 2 * zone * row_count, CHUNK)
        return left.at[pl.ds(chan, count), pl.ds(first, zone * row_count), :]

    def pass_early(from_q, chunk, to_q, came, landed):
        await_part(right_rows(0, early, 0, zone * CHUNK), came)
        for to_lane in range(zone):
            first = (from_q * zone + to_lane) * row_count + chunk * CHUNK
            pass_on(right_rows(0, early, first, CHUNK), to_q, landed)

    def pass_late(from_q, group, to_q, came, landed):
        part = right_rows(early + group, 1, from_q * zone * row_count, zone * row_count)
        await_part(part, came)
        pass_on(part, to_q, landed)

    def pass_left(chan, count, group):
        part = left_rows(chan, count, quarter)
        await_part(part, recv_left.at[0, group])
        pass_on(part, hub_q, recv_left.at[1, group])

    def pass_first(chunk):
        @pl.when(inner)
        def _():
            pass_early(quarter, chunk, far_q, recv_early.at[0, chunk], recv_far.at[0])

        @pl.when(place == 1)
        def _():
            pass_early(quarter, chunk, hub_q, recv_early.at[0, chunk], recv_early.at[1, chunk])

    def cross_near(group):
        pass_late(hub_q, group, far_q, recv_right.at[0, group], recv_far.at[1 + group])

    def cross_edge(group):
        pass_late(edge_q, group, far_q, recv_right.at[1, group], recv_far.at[1 + group])

    def climb(group, carry):
        pass_late(edge_q, group, hub_q, recv_right.at[0, group], recv_right.at[1, group])
        pass_left(early + group, 1, 1 + group)
        return carry

    def triangle(chan, count, group):
        await_part(left_rows(chan, count, hub_q), recv_left.at[0, group])
        await_part(left_rows(chan, count, edge_q), recv_left.at[1, group])
        await_part(right_rows(chan, count, 0, group_rows * row_count), recv_far.at[group])

        def one_channel(at, carry):
            tri[at] = lax.dot_general(
                left[at], right[at], (((1,), (1,)), ((), ())), preferred_element_type=jnp.float32
            ).astype(jnp.bfloat16)
            return carry

        lax.fori_loop(chan, chan + count, one_channel, 0)
        slot = back.at[pl.ds(member * share + chan, count)]

        def tri_part(to_spot, to_col):
            return tri.at[
                pl.ds(chan, count),
                pl.ds(pl.multiple_of(to_spot * row_count, CHUNK), row_count),
                pl.ds(pl.multiple_of(to_col * col_count, 128), col_count),
            ]

        def give(step, carry):
            to_spot, to_col = (spot + step % group_rows) % group_rows, (col + step // group_rows) % ka_n
            pltpu.make_async_remote_copy(
                src_ref=tri_part(to_spot, to_col), dst_ref=slot,
                send_sem=send_tri, recv_sem=recv_tri,
                device_id=(half * group_rows + to_spot, to_col), device_id_type=MESH,
            ).start()
            return carry

        lax.fori_loop(1, members, give, 0)
        pltpu.make_async_copy(tri_part(spot, col), slot, recv_tri).start()

    make_chunk(0)
    pl.semaphore_wait(barrier, rows_n * ka_n - 1)
    send_early(0)

    def rest(chunk, carry):
        make_chunk(chunk)
        send_early(chunk)
        pass_first(chunk - 1)
        return carry

    lax.fori_loop(1, chunks, rest, 0)
    pass_first(chunks - 1)

    @pl.when(place == 1)
    def _():
        pass_left(0, early, 0)

    lax.fori_loop(0, late, send_late, 0)

    @pl.when(inner)
    def _():
        for chunk in range(chunks):
            pass_early(edge_q, chunk, far_q, recv_early.at[1, chunk], recv_far.at[0])
        cross_near(0)
        cross_near(1)

    @pl.when(place == 1)
    def _():
        climb(0, 0)
        climb(1, 0)

    gain_col[...] = jnp.broadcast_to(out_gain_ref[...], (col_count, hidden)).T
    bias_col[...] = jnp.broadcast_to(out_bias_ref[...], (col_count, hidden)).T

    def gate_row(at, carry):
        gates[at] = sigmoid(
            jnp.dot(normed[at], w_out_gate_ref[...], preferred_element_type=jnp.float32)
        )
        return carry

    lax.fori_loop(0, row_count, gate_row, 0, unroll=GATE_UNROLL)

    @pl.when(place == 1)
    def _():
        lax.fori_loop(2, late, climb, 0)

    @pl.when(inner)
    def _():
        cross_near(2)
        cross_edge(0)
        triangle(0, early, 0)

        def stage(group, carry):
            @pl.when(group + 2 < late)
            def _():
                cross_near(group + 2)

            cross_edge(group)
            triangle(early + group - 1, 1, group)
            return carry

        lax.fori_loop(1, late, stage, 0)
        triangle(share - 1, 1, late)

    pltpu.make_async_copy(back, back, recv_tri).wait()

    def finish(chunk, carry):
        first = pl.multiple_of(chunk * CHUNK, CHUNK)
        sums = back[:, pl.ds(first, CHUNK), :].astype(jnp.float32)
        center = jnp.mean(sums, axis=0, keepdims=True)
        deviate = sums - center
        spread = jnp.mean(deviate * deviate, axis=0, keepdims=True)
        scaled = deviate * lax.rsqrt(spread + 1e-05)
        planes[:hidden, :CHUNK, :] = scaled

        def one_row(local, inner_carry):
            at = first + local
            chans_first = wide[pl.ds(local, hidden, stride=PITCH), :]
            tri_normed = (chans_first * gain_col[...] + bias_col[...]).astype(jnp.bfloat16)
            projected = lax.dot_general(
                tri_normed, w_out_ref[...], (((0,), (0,)), ((), ())), preferred_element_type=jnp.float32
            )
            out_ref[at] = (gates[at] * projected).astype(jnp.bfloat16)
            return inner_carry

        lax.fori_loop(0, CHUNK, one_row, 0, unroll=FINISH_UNROLL)
        pltpu.make_async_copy(
            out_ref.at[chunk_rows(chunk)], out_hbm.at[chunk_rows(chunk)], store_sem
        ).start()
        return carry

    lax.fori_loop(0, chunks, finish, 0)
    pltpu.make_async_copy(out_ref, out_hbm, store_sem).wait()

    others = edges.at[pl.ds(0, (hubs - 1) * share)]
    pltpu.make_async_copy(others, others, send_left).wait()
    pltpu.make_async_copy(others, others, send_right).wait()

    passed = right.at[:, pl.ds(0, group_rows * row_count), :]
    pltpu.make_async_copy(passed, passed, send_far).wait()

    @pl.when(inner)
    def _():
        most = tri.at[:, pl.ds(0, (group_rows - 1) * row_count), :]
        pltpu.make_async_copy(most, most, send_tri).wait()
        more = tri.at[:, pl.ds(0, row_count), pl.ds(0, (ka_n - 1) * col_count)]
        pltpu.make_async_copy(more, more, send_tri).wait()


def fused(rows_n, ka_n, args):
    pair_repr, pair_mask, ln_gain, ln_bias, w_proj, w_gate, w_out_gate, out_gain, out_bias, w_out = args
    row_count, col_count, chans = pair_repr.shape
    hidden = w_out.shape[0]
    share = hidden // (rows_n // 4 * ka_n)
    late = share - EARLY
    chunks = row_count // CHUNK
    half = jnp.bfloat16
    return pl.pallas_call(
        functools.partial(kernel, rows_n, ka_n, EARLY),
        out_shape=jax.ShapeDtypeStruct(pair_repr.shape, half),
        in_specs=[pl.BlockSpec(memory_space=pl.ANY)] + [pl.BlockSpec(memory_space=pltpu.VMEM)] * 9,
        out_specs=pl.BlockSpec(memory_space=pl.ANY),
        scratch_shapes=[
            pltpu.VMEM((row_count, col_count, chans), half),
            pltpu.VMEM((row_count, col_count, chans), half),
            pltpu.VMEM((2 * hidden, row_count, col_count), half),
            pltpu.VMEM((2 * hidden * PITCH, col_count), jnp.float32),
            pltpu.VMEM((row_count, col_count, chans), half),
            pltpu.VMEM((row_count, col_count, chans), jnp.float32),
            pltpu.VMEM((share, rows_n // 2 * row_count, ka_n * col_count), half),
            pltpu.VMEM((share, rows_n * row_count, ka_n * col_count), half),
            pltpu.VMEM((share, rows_n // 2 * row_count, ka_n * col_count), half),
            pltpu.VMEM((hidden, row_count, col_count), half),
            pltpu.VMEM((4 * hidden, chans), half),
            pltpu.VMEM((hidden, col_count), jnp.float32),
            pltpu.VMEM((hidden, col_count), jnp.float32),
            pltpu.SemaphoreType.DMA((chunks,)),
            pltpu.SemaphoreType.DMA,
            pltpu.SemaphoreType.DMA((2, 1 + late)),
            pltpu.SemaphoreType.DMA((2, chunks)),
            pltpu.SemaphoreType.DMA((2, late)),
            pltpu.SemaphoreType.DMA((1 + late,)),
            pltpu.SemaphoreType.DMA,
            pltpu.SemaphoreType.DMA,
            pltpu.SemaphoreType.DMA,
            pltpu.SemaphoreType.DMA,
            pltpu.SemaphoreType.DMA,
        ],
        compiler_params=pltpu.CompilerParams(
            collective_id=0, has_side_effects=True, vmem_limit_bytes=60 * 2**20
        ),
    )(
        pair_repr, pair_mask, ln_gain[None], ln_bias[None], w_proj, w_gate, w_out_gate,
        out_gain[None], out_bias[None], w_out,
    )


def plain(args):
    pair_repr, pair_mask, ln_gain, ln_bias, w_proj, w_gate, w_out_gate, out_gain, out_bias, w_out = args
    row_count, col_count, chans = pair_repr.shape
    hidden = w_out.shape[0]
    normed = layer_norm(pair_repr.astype(jnp.float32), ln_gain, ln_bias).astype(jnp.bfloat16)
    flat_rows = normed.reshape(row_count * col_count, chans)
    projected = jnp.dot(flat_rows, w_proj, preferred_element_type=jnp.float32)
    gate_logits = jnp.dot(flat_rows, w_gate, preferred_element_type=jnp.float32)
    mask_col = pair_mask.reshape(row_count * col_count, 1).astype(jnp.float32)
    edges = (jax.nn.sigmoid(gate_logits) * projected * mask_col).astype(jnp.bfloat16)
    edges = edges.reshape(row_count, col_count, 2 * hidden)
    partial_sums = jnp.einsum(
        "ikh,jkh->ijh",
        edges[:, :, :hidden],
        lax.all_gather(edges[:, :, hidden:], "rows", axis=0, tiled=True),
        preferred_element_type=jnp.float32,
    )
    triangle = lax.psum_scatter(
        partial_sums.astype(jnp.bfloat16), "ka", scatter_dimension=1, tiled=True
    ).astype(jnp.float32)
    tri_normed = layer_norm(triangle, out_gain, out_bias).astype(jnp.bfloat16)
    out_gate = jax.nn.sigmoid(jnp.dot(flat_rows, w_out_gate, preferred_element_type=jnp.float32))
    projected_out = jnp.dot(
        tri_normed.reshape(row_count * col_count, hidden), w_out, preferred_element_type=jnp.float32
    )
    return (out_gate * projected_out).astype(jnp.bfloat16).reshape(row_count, col_count, chans)


def body(rows_n, ka_n, *args):
    row_count, col_count, chans = args[0].shape
    hidden = args[-1].shape[0]
    hubs = rows_n // 4 * ka_n
    aligned = row_count % CHUNK == 0 and col_count % 128 == 0 and chans % 128 == 0 and hidden % 128 == 0
    if aligned and rows_n % 4 == 0 and hidden % hubs == 0 and col_count == hidden:
        if hidden // hubs - EARLY > max(2, row_count // CHUNK):
            return fused(rows_n, ka_n, args)
    return plain(args)


def solution(mesh):
    placed = (P("rows", "ka", None), P("rows", "ka"), P(), P(), P(), P(), P(), P(), P(), P())
    return jax.shard_map(
        functools.partial(body, mesh.shape["rows"], mesh.shape["ka"]),
        mesh=mesh, in_specs=placed, out_specs=P("rows", "ka", None), check_vma=False,
    )
```

time: 132 us -> 123 us (0.932); the launches traced: 130 us -> 123 us
  Pallas kernels: 126 us -> 120 us
    pallas_call x1, Pallas kernels: 126 us -> 120 us  [fused(): pl.pallas_call(functools.partial(kernel, rows_n, ka_n, EARLY), out_shape=...]
where the time goes in v1:
time: 123 us
  Pallas kernels  120 us (98%)
  local copies, waits for them, and re-layouts  3.16 us (3%)
    pallas_call x1, Pallas kernels, fused(): pl.pallas_call(functools.partial(kernel, rows_n, ka_n, EARLY), out_shape=...  120 us
    unnamed x1, local copies, waits for them, and re-layouts  3.16 us

profile of v1, /device:TPU:0, one launch (start us, length us, event | category | flops | bytes accessed | tf_op | source)
XLA Modules:
  0.0 123.0 jit_solution(17614474982956648093)
XLA Ops:
  0.0 119.9 %shard_map.100 = bf16[64,128,128]{2,1,0:T(8,128)(2,1)} custom-call(bf16[64,128,128]{2,1,0:T(8,128)(2,1)} %pair_hbm.1, s32[64,128]{1,0:T(8,128)} %mask_ref.1, f32[1,128]{1,0:T(1,128)} %bitcast.4, f32[1,128]{1,0:T(1,128)} %bitcast.5, bf16[128,256]{1,0:T(8,128)(2,1)} %w_proj_ref.1, bf16[128,256]{1,0:T(8,128)(2,1)} %w_gate_ref.1, ...), custom_call_target="tpu_custom_call" | custom-call | tf_op jit(solution)/shard_map/pallas_call | solution.py:351
  119.9 3.2 %copy.12 = bf16[64,128,128]{2,1,0:T(8,128)(2,1)} copy(bf16[64,128,128]{2,1,0:T(8,128)(2,1)} %shard_map.100) | data formatting | bytes 4194304

commit v2 on v1

--- a/solution.py
+++ b/solution.py
@@ -10,7 +10,8 @@
 MESH = pl.DeviceIdType.MESH
 CHUNK = 16
 PITCH = 24
-EARLY = 2
+EARLY = 4
+AHEAD = 3
 MAKE_UNROLL = 8
 GATE_UNROLL = 8
 FINISH_UNROLL = 16
@@ -29,17 +30,19 @@
 
 def kernel(
     rows_n, ka_n, early,
-    pair_hbm, mask_ref, ln_gain_ref, ln_bias_ref, w_proj_ref, w_gate_ref, w_out_gate_ref,
+    pair_hbm, mask_hbm, ln_gain_hbm, ln_bias_hbm, w_proj_hbm, w_gate_hbm, w_out_gate_hbm,
+    out_gain_hbm, out_bias_hbm, w_out_hbm,
+    out_hbm,
+    mask_ref, ln_gain_ref, ln_bias_ref, w_proj_ref, w_gate_ref, w_out_gate_ref,
     out_gain_ref, out_bias_ref, w_out_ref,
-    out_hbm,
     pair_ref, out_ref, edges, wide, normed, gates, left, right, tri, back, w_cat, gain_col, bias_col,
-    load_sem, store_sem, recv_left, recv_early, recv_right, recv_far, recv_tri,
+    small_sem, load_sem, store_sem, recv_left, recv_first, recv_early, recv_own, recv_right, recv_far, recv_tri,
     send_left, send_right, send_far, send_tri,
 ):
     row = lax.axis_index("rows")
     col = lax.axis_index("ka")
     row_count, col_count, chans = pair_ref.shape
-    hidden = w_out_ref.shape[0]
+    hidden = w_out_hbm.shape[0]
     zone = rows_n // 4
     group_rows = 2 * zone
     members = group_rows * ka_n
@@ -47,6 +50,7 @@
     share = hidden // hubs
     late = share - early
     chunks = row_count // CHUNK
+    ahead = AHEAD
 
     quarter = row // zone
     lane = row % zone
@@ -67,7 +71,20 @@
         rows = chunk_rows(chunk)
         return pltpu.make_async_copy(pair_hbm.at[rows], pair_ref.at[rows], load_sem.at[chunk])
 
-    for chunk in range(chunks):
+    smalls = [
+        pltpu.make_async_copy(there, here, small_sem.at[at])
+        for at, (there, here) in enumerate([
+            (w_gate_hbm, w_gate_ref), (w_proj_hbm, w_proj_ref), (ln_gain_hbm, ln_gain_ref),
+            (ln_bias_hbm, ln_bias_ref), (mask_hbm, mask_ref), (w_out_gate_hbm, w_out_gate_ref),
+            (out_gain_hbm, out_gain_ref), (out_bias_hbm, out_bias_ref), (w_out_hbm, w_out_ref),
+        ])
+    ]
+    smalls[0].start()
+    smalls[1].start()
+    load(0).start()
+    for small in smalls[2:]:
+        small.start()
+    for chunk in range(1, chunks):
         load(chunk).start()
 
     barrier = pltpu.get_barrier_semaphore()
@@ -83,6 +100,8 @@
     def turned(ref):
         return ref[...].astype(jnp.float32).T.astype(jnp.bfloat16)
 
+    smalls[0].wait()
+    smalls[1].wait()
     w_cat[: 2 * hidden, :] = turned(w_gate_ref)
     w_cat[2 * hidden :, :] = turned(w_proj_ref)
 
@@ -100,18 +119,21 @@
             right.at[pl.ds(chan, count), pl.ds(row * row_count + first, size), own_cols],
         )
 
-    def send_edges(ends, chan, count, first, size, sent, landed):
+    def send_edges(ends, chan, count, first, size, sent, landed, to_q=None):
         def start(to_lane, to_col):
             here, there = ends(chan, count, first, size, to_lane * ka_n + to_col)
             pltpu.make_async_remote_copy(
                 src_ref=here, dst_ref=there, send_sem=sent, recv_sem=landed,
-                device_id=(quarter * zone + to_lane, to_col), device_id_type=MESH,
+                device_id=((quarter if to_q is None else to_q) * zone + to_lane, to_col), device_id_type=MESH,
             ).start()
 
         def other(step, carry):
             start((lane + step % zone) % zone, (col + step // zone) % ka_n)
             return carry
 
+        if to_q is not None:
+            lax.fori_loop(0, hubs, other, 0)
+            return
         lax.fori_loop(1, hubs, other, 0)
         here, there = ends(chan, count, first, size, member)
         pltpu.make_async_copy(here, there, landed).start()
@@ -137,14 +159,32 @@
 
     def send_early(chunk):
         first = pl.multiple_of(chunk * CHUNK, CHUNK)
-        send_edges(right_ends, 0, early, first, CHUNK, send_right, recv_early.at[0, chunk])
-        send_edges(left_ends, 0, early, first, CHUNK, send_left, recv_left.at[0, 0])
-
-    def send_late(group, carry):
-        chan = early + group
-        send_edges(right_ends, chan, 1, 0, row_count, send_right, recv_right.at[0, group])
-        send_edges(left_ends, chan, 1, 0, row_count, send_left, recv_left.at[0, 1 + group])
-        return carry
+
+        @pl.when(inner)
+        def _():
+            send_edges(right_ends, 0, early, first, CHUNK, send_far, recv_far.at[0], far_q)
+
+        @pl.when(place == 1)
+        def _():
+            @pl.when(chunk == 0)
+            def _():
+                send_edges(right_ends, 0, early, first, CHUNK, send_far, recv_early.at[0], hub_q)
+
+            @pl.when(chunk > 0)
+            def _():
+                send_edges(right_ends, 0, early, first, CHUNK, send_right, recv_first.at[0, chunk])
+
+            send_edges(left_ends, 0, early, first, CHUNK, send_left, recv_first.at[1, chunk])
+
+    def send_right_late(group):
+        send_edges(right_ends, early + group, 1, 0, row_count, send_right, recv_right.at[0, group])
+
+    def send_left_late(group):
+        send_edges(left_ends, early + group, 1, 0, row_count, send_left, recv_left.at[0, 1 + group])
+
+    def send_both(group, lead):
+        send_right_late(group + lead)
+        send_left_late(group)
 
     def await_part(part, landed):
         pltpu.make_async_copy(part, part, landed).wait()
@@ -162,8 +202,7 @@
         first = pl.multiple_of(from_q % 2 * zone * row_count, CHUNK)
         return left.at[pl.ds(chan, count), pl.ds(first, zone * row_count), :]
 
-    def pass_early(from_q, chunk, to_q, came, landed):
-        await_part(right_rows(0, early, 0, zone * CHUNK), came)
+    def pass_early(from_q, chunk, to_q, landed):
         for to_lane in range(zone):
             first = (from_q * zone + to_lane) * row_count + chunk * CHUNK
             pass_on(right_rows(0, early, first, CHUNK), to_q, landed)
@@ -178,14 +217,23 @@
         await_part(part, recv_left.at[0, group])
         pass_on(part, hub_q, recv_left.at[1, group])
 
-    def pass_first(chunk):
-        @pl.when(inner)
+    def climb_early(chunk):
+        sizer = right_rows(0, early, 0, zone * CHUNK)
+
+        @pl.when(chunk > 0)
         def _():
-            pass_early(quarter, chunk, far_q, recv_early.at[0, chunk], recv_far.at[0])
-
-        @pl.when(place == 1)
-        def _():
-            pass_early(quarter, chunk, hub_q, recv_early.at[0, chunk], recv_early.at[1, chunk])
+            await_part(sizer, recv_first.at[0, chunk])
+            pass_early(quarter, chunk, hub_q, recv_early.at[chunk])
+
+        await_part(sizer, recv_first.at[1, chunk])
+        for to_lane in range(zone):
+            first = (quarter % 2 * zone + to_lane) * row_count + chunk * CHUNK
+            rows = pl.ds(pl.multiple_of(first, CHUNK), CHUNK)
+            pass_on(left.at[pl.ds(0, early), rows, :], hub_q, recv_left.at[1, 0])
+
+    def cross_early(chunk):
+        await_part(right_rows(0, early, 0, zone * CHUNK), recv_early.at[chunk])
+        pass_early(edge_q, chunk, far_q, recv_far.at[0])
 
     def cross_near(group):
         pass_late(hub_q, group, far_q, recv_right.at[0, group], recv_far.at[1 + group])
@@ -193,9 +241,15 @@
     def cross_edge(group):
         pass_late(edge_q, group, far_q, recv_right.at[1, group], recv_far.at[1 + group])
 
+    def climb_right(group):
+        pass_late(edge_q, group, hub_q, recv_right.at[0, group], recv_right.at[1, group])
+
+    def climb_left(group):
+        pass_left(early + group, 1, 1 + group)
+
     def climb(group, carry):
-        pass_late(edge_q, group, hub_q, recv_right.at[0, group], recv_right.at[1, group])
-        pass_left(early + group, 1, 1 + group)
+        climb_right(group)
+        climb_left(group - 1)
         return carry
 
     def triangle(chan, count, group):
@@ -231,6 +285,8 @@
         lax.fori_loop(1, members, give, 0)
         pltpu.make_async_copy(tri_part(spot, col), slot, recv_tri).start()
 
+    for small in smalls[2:]:
+        small.wait()
     make_chunk(0)
     pl.semaphore_wait(barrier, rows_n * ka_n - 1)
     send_early(0)
@@ -238,29 +294,48 @@
     def rest(chunk, carry):
         make_chunk(chunk)
         send_early(chunk)
-        pass_first(chunk - 1)
+
+        @pl.when(place == 1)
+        def _():
+            climb_early(chunk - 1)
+
         return carry
 
     lax.fori_loop(1, chunks, rest, 0)
-    pass_first(chunks - 1)
 
     @pl.when(place == 1)
     def _():
-        pass_left(0, early, 0)
-
-    lax.fori_loop(0, late, send_late, 0)
+        climb_early(chunks - 1)
+        send_right_late(0)
+
+        def both(group, carry):
+            send_both(group, 1)
+            return carry
+
+        lax.fori_loop(0, late - 1, both, 0)
+        send_left_late(late - 1)
+        climb_right(0)
+        climb(1, 0)
 
     @pl.when(inner)
     def _():
+        for group in range(ahead):
+            send_right_late(group)
+        send_edges(right_ends, 0, early, 0, row_count, send_right, recv_own)
+        send_edges(left_ends, 0, early, 0, row_count, send_left, recv_left.at[0, 0])
         for chunk in range(chunks):
-            pass_early(edge_q, chunk, far_q, recv_early.at[1, chunk], recv_far.at[0])
-        cross_near(0)
-        cross_near(1)
-
-    @pl.when(place == 1)
-    def _():
-        climb(0, 0)
-        climb(1, 0)
+            cross_early(chunk)
+
+            def both(group, carry):
+                send_both(group, ahead)
+                return carry
+
+            span = late - ahead
+            lax.fori_loop(span * chunk // chunks, span * (chunk + 1) // chunks, both, 0)
+            if chunk < ahead:
+                cross_near(chunk)
+        for group in range(late - ahead, late):
+            send_left_late(group)
 
     gain_col[...] = jnp.broadcast_to(out_gain_ref[...], (col_count, hidden)).T
     bias_col[...] = jnp.broadcast_to(out_bias_ref[...], (col_count, hidden)).T
@@ -276,17 +351,20 @@
     @pl.when(place == 1)
     def _():
         lax.fori_loop(2, late, climb, 0)
+        climb_left(late - 1)
 
     @pl.when(inner)
     def _():
-        cross_near(2)
+        for group in range(min(chunks, ahead), ahead + 1):
+            cross_near(group)
         cross_edge(0)
+        await_part(right_rows(0, early, hub_q * zone * row_count, zone * row_count), recv_own)
         triangle(0, early, 0)
 
         def stage(group, carry):
-            @pl.when(group + 2 < late)
+            @pl.when(group + ahead < late)
             def _():
-                cross_near(group + 2)
+                cross_near(group + ahead)
 
             cross_edge(group)
             triangle(early + group - 1, 1, group)
@@ -325,12 +403,20 @@
     lax.fori_loop(0, chunks, finish, 0)
     pltpu.make_async_copy(out_ref, out_hbm, store_sem).wait()
 
-    others = edges.at[pl.ds(0, (hubs - 1) * share)]
-    pltpu.make_async_copy(others, others, send_left).wait()
-    pltpu.make_async_copy(others, others, send_right).wait()
+    def sent_all(first, count, rows, sem):
+        part = edges.at[pl.ds(0, count), pl.ds(first, rows), :]
+        await_part(part, sem)
+
+    sent_all(0, (hubs - 1) * share, row_count, send_left)
+    sent_all(0, (hubs - 1) * late, row_count, send_right)
+    sent_all(CHUNK, (hubs - 1) * early, row_count - CHUNK, send_right)
+
+    @pl.when(inner)
+    def _():
+        sent_all(0, (hubs - 1) * early, CHUNK, send_right)
 
     passed = right.at[:, pl.ds(0, group_rows * row_count), :]
-    pltpu.make_async_copy(passed, passed, send_far).wait()
+    await_part(passed, send_far)
 
     @pl.when(inner)
     def _():
@@ -351,9 +437,18 @@
     return pl.pallas_call(
         functools.partial(kernel, rows_n, ka_n, EARLY),
         out_shape=jax.ShapeDtypeStruct(pair_repr.shape, half),
-        in_specs=[pl.BlockSpec(memory_space=pl.ANY)] + [pl.BlockSpec(memory_space=pltpu.VMEM)] * 9,
+        in_specs=[pl.BlockSpec(memory_space=pltpu.HBM)] * 10,
         out_specs=pl.BlockSpec(memory_space=pl.ANY),
         scratch_shapes=[
+            pltpu.VMEM((row_count, col_count), jnp.int32),
+            pltpu.VMEM((1, chans), jnp.float32),
+            pltpu.VMEM((1, chans), jnp.float32),
+            pltpu.VMEM((chans, 2 * hidden), half),
+            pltpu.VMEM((chans, 2 * hidden), half),
+            pltpu.VMEM((chans, chans), half),
+            pltpu.VMEM((1, hidden), jnp.float32),
+            pltpu.VMEM((1, hidden), jnp.float32),
+            pltpu.VMEM((hidden, chans), half),
             pltpu.VMEM((row_count, col_count, chans), half),
             pltpu.VMEM((row_count, col_count, chans), half),
             pltpu.VMEM((2 * hidden, row_count, col_count), half),
@@ -367,10 +462,13 @@
             pltpu.VMEM((4 * hidden, chans), half),
             pltpu.VMEM((hidden, col_count), jnp.float32),
             pltpu.VMEM((hidden, col_count), jnp.float32),
+            pltpu.SemaphoreType.DMA((9,)),
             pltpu.SemaphoreType.DMA((chunks,)),
             pltpu.SemaphoreType.DMA,
             pltpu.SemaphoreType.DMA((2, 1 + late)),
             pltpu.SemaphoreType.DMA((2, chunks)),
+            pltpu.SemaphoreType.DMA((chunks,)),
+            pltpu.SemaphoreType.DMA,
             pltpu.SemaphoreType.DMA((2, late)),
             pltpu.SemaphoreType.DMA((1 + late,)),
             pltpu.SemaphoreType.DMA,
@@ -380,12 +478,15 @@
             pltpu.SemaphoreType.DMA,
         ],
         compiler_params=pltpu.CompilerParams(
-            collective_id=0, has_side_effects=True, vmem_limit_bytes=60 * 2**20
+            collective_id=0, has_side_effects=True, vmem_limit_bytes=42 * 2**20
         ),
-    )(
-        pair_repr, pair_mask, ln_gain[None], ln_bias[None], w_proj, w_gate, w_out_gate,
-        out_gain[None], out_bias[None], w_out,
-    )
+    )(*[
+        pltpu.with_memory_space_constraint(array, pltpu.HBM)
+        for array in (
+            pair_repr, pair_mask, ln_gain[None], ln_bias[None], w_proj, w_gate, w_out_gate,
+            out_gain[None], out_bias[None], w_out,
+        )
+    ])
 
 
 def plain(args):
@@ -422,7 +523,7 @@
     hubs = rows_n // 4 * ka_n
     aligned = row_count % CHUNK == 0 and col_count % 128 == 0 and chans % 128 == 0 and hidden % 128 == 0
     if aligned and rows_n % 4 == 0 and hidden % hubs == 0 and col_count == hidden:
-        if hidden // hubs - EARLY > max(2, row_count // CHUNK):
+        if hidden // hubs - EARLY > AHEAD and row_count > CHUNK:
             return fused(rows_n, ka_n, args)
     return plain(args)
 

time: 123 us -> 111 us (0.902)
  Pallas kernels: 120 us -> 109 us
  local copies, waits for them, and re-layouts: 3.16 us -> 1.32 us
    pallas_call x1, Pallas kernels: 120 us -> 109 us  [fused(): pl.pallas_call(functools.partial(kernel, rows_n, ka_n, EARLY), out_shape=...]
    unnamed x1, local copies, waits for them, and re-layouts: 3.16 us -> 1.32 us
where the time goes in v2:
time: 111 us
  Pallas kernels  109 us (98%)
  local copies, waits for them, and re-layouts  1.32 us (1%)
    pallas_call x1, Pallas kernels, fused(): pl.pallas_call(functools.partial(kernel, rows_n, ka_n, EARLY), out_shape=...  109 us

profile of v2, /device:TPU:0, one launch (start us, length us, event | category | flops | bytes accessed | tf_op | source)
XLA Modules:
  0.0 110.7 jit_solution(9596678739879741892)
XLA Ops:
  0.0 109.4 %shard_map.100 = bf16[64,128,128]{2,1,0:T(8,128)(2,1)S(1)} custom-call(bf16[64,128,128]{2,1,0:T(8,128)(2,1)} %pair_hbm.1, s32[64,128]{1,0:T(8,128)} %mask_hbm.1, f32[1,128]{1,0:T(1,128)} %bitcast.4, f32[1,128]{1,0:T(1,128)} %bitcast.5, bf16[128,256]{1,0:T(8,128)(2,1)} %w_proj_hbm.1, bf16[128,256]{1,0:T(8,128)(2,1)} %w_gate_hbm.1, ...), custom_call_target="tpu_custom_call" | custom-call | tf_op jit(solution)/shard_map/pallas_call | solution.py:437
  109.4 1.3 %copy.12 = bf16[64,128,128]{2,1,0:T(8,128)(2,1)} copy(bf16[64,128,128]{2,1,0:T(8,128)(2,1)S(1)} %shard_map.100) | data formatting | bytes 4194304

commit v3 on v2

--- a/solution.py
+++ b/solution.py
@@ -11,6 +11,7 @@
 CHUNK = 16
 PITCH = 24
 EARLY = 4
+SHARED = 2
 AHEAD = 3
 MAKE_UNROLL = 8
 GATE_UNROLL = 8
@@ -35,8 +36,9 @@
     out_hbm,
     mask_ref, ln_gain_ref, ln_bias_ref, w_proj_ref, w_gate_ref, w_out_gate_ref,
     out_gain_ref, out_bias_ref, w_out_ref,
-    pair_ref, out_ref, edges, wide, normed, gates, left, right, tri, back, w_cat, gain_col, bias_col,
-    small_sem, load_sem, store_sem, recv_left, recv_first, recv_early, recv_own, recv_right, recv_far, recv_tri,
+    pair_ref, out_ref, edges, wide, normed, gates, left, right, tri, back, w_cat, w_scaled, bias_row,
+    mean_part, square_part,
+    small_sem, load_sem, store_sem, recv_left, recv_first, recv_early, recv_own, recv_down, recv_right, recv_far, recv_tri,
     send_left, send_right, send_far, send_tri,
 ):
     row = lax.axis_index("rows")
@@ -51,6 +53,7 @@
     late = share - early
     chunks = row_count // CHUNK
     ahead = AHEAD
+    shared = SHARED
 
     quarter = row // zone
     lane = row % zone
@@ -63,6 +66,19 @@
     inner = place == 0
     member = lane * ka_n + col
     planes = wide.reshape(2 * hidden, PITCH, col_count)
+
+    barrier = pltpu.get_barrier_semaphore()
+
+    def hail(to_row, to_col):
+        pl.semaphore_signal(barrier, inc=1, device_id=(to_row, to_col), device_id_type=MESH)
+
+    def greet(step, carry):
+        hail(half * group_rows + (spot + step % group_rows) % group_rows, (col + step // group_rows) % ka_n)
+        return carry
+
+    def greet_far(step, carry):
+        hail(far_q * zone + step % zone, (col + step // zone) % ka_n)
+        return carry
 
     def chunk_rows(chunk):
         return pl.ds(pl.multiple_of(chunk * CHUNK, CHUNK), CHUNK)
@@ -87,23 +103,22 @@
     for chunk in range(1, chunks):
         load(chunk).start()
 
-    barrier = pltpu.get_barrier_semaphore()
-
-    def greet(step, carry):
-        to_row = (row + step // ka_n) % rows_n
-        to_col = (col + step % ka_n) % ka_n
-        pl.semaphore_signal(barrier, inc=1, device_id=(to_row, to_col), device_id_type=MESH)
-        return carry
-
-    lax.fori_loop(1, rows_n * ka_n, greet, 0)
+    @pl.when(inner)
+    def _():
+        lax.fori_loop(0, hubs, greet_far, 0)
+
+    lax.fori_loop(1, members, greet, 0)
 
     def turned(ref):
         return ref[...].astype(jnp.float32).T.astype(jnp.bfloat16)
 
     smalls[0].wait()
     smalls[1].wait()
-    w_cat[: 2 * hidden, :] = turned(w_gate_ref)
-    w_cat[2 * hidden :, :] = turned(w_proj_ref)
+    gate_rows, proj_rows = turned(w_gate_ref), turned(w_proj_ref)
+    w_cat[:hidden, :] = gate_rows[hidden:]
+    w_cat[hidden : 2 * hidden, :] = proj_rows[hidden:]
+    w_cat[2 * hidden : 3 * hidden, :] = gate_rows[:hidden]
+    w_cat[3 * hidden :, :] = proj_rows[:hidden]
 
     own_cols = pl.ds(pl.multiple_of(col * col_count, 128), col_count)
 
@@ -138,42 +153,72 @@
         here, there = ends(chan, count, first, size, member)
         pltpu.make_async_copy(here, there, landed).start()
 
+    def make_side(at, local, plain, first_row, first_chan):
+        both = lax.dot_general(
+            w_cat[first_row : first_row + 2 * hidden], plain, (((1,), (1,)), ((), ())),
+            preferred_element_type=jnp.float32,
+        )
+        mask_row = mask_ref[pl.ds(at, 1), :].astype(jnp.float32)
+        made = sigmoid(both[:hidden]) * both[hidden:] * mask_row
+        wide[pl.ds(local + first_chan * PITCH, hidden, stride=PITCH), :] = made
+
+    def normalise(at):
+        values = pair_ref[at].astype(jnp.float32)
+        plain = layer_norm(values, ln_gain_ref[...], ln_bias_ref[...]).astype(jnp.bfloat16)
+        normed[at] = plain
+        return plain
+
+    def round_side(chunk, first_chan, count):
+        some = pl.ds(first_chan, count)
+        edges[some, chunk_rows(chunk), :] = planes[some, :CHUNK, :].astype(jnp.bfloat16)
+
+    def make_first():
+        load(0).wait()
+
+        def right_row(at, carry):
+            make_side(at, at, normalise(at), 0, hidden)
+            return carry
+
+        lax.fori_loop(0, CHUNK, right_row, 0, unroll=MAKE_UNROLL)
+        round_side(0, hidden, hidden)
+
+    def make_first_left():
+        def left_row(at, carry):
+            make_side(at, at, normed[at], 2 * hidden, 0)
+            return carry
+
+        lax.fori_loop(0, CHUNK, left_row, 0, unroll=MAKE_UNROLL)
+        round_side(0, 0, hidden)
+
     def make_chunk(chunk):
         load(chunk).wait()
 
         def one_row(local, carry):
             at = chunk * CHUNK + local
-            values = pair_ref[at].astype(jnp.float32)
-            plain = layer_norm(values, ln_gain_ref[...], ln_bias_ref[...]).astype(jnp.bfloat16)
-            normed[at] = plain
-            both = lax.dot_general(
-                w_cat[...], plain, (((1,), (1,)), ((), ())), preferred_element_type=jnp.float32
-            )
-            mask_row = mask_ref[pl.ds(at, 1), :].astype(jnp.float32)
-            made = sigmoid(both[: 2 * hidden]) * both[2 * hidden :] * mask_row
-            wide[pl.ds(local, 2 * hidden, stride=PITCH), :] = made
+            plain = normalise(at)
+            make_side(at, local, plain, 0, hidden)
+            make_side(at, local, plain, 2 * hidden, 0)
             return carry
 
         lax.fori_loop(0, CHUNK, one_row, 0, unroll=MAKE_UNROLL)
-        edges[:, chunk_rows(chunk), :] = planes[:, :CHUNK, :].astype(jnp.bfloat16)
-
-    def send_early(chunk):
+        round_side(chunk, 0, 2 * hidden)
+
+    def send_early_right(chunk):
         first = pl.multiple_of(chunk * CHUNK, CHUNK)
 
         @pl.when(inner)
         def _():
             send_edges(right_ends, 0, early, first, CHUNK, send_far, recv_far.at[0], far_q)
 
+        @pl.when((place == 1) & (chunk > 0))
+        def _():
+            send_edges(right_ends, 0, early, first, CHUNK, send_right, recv_first.at[0, chunk])
+
+    def send_early_left(chunk):
+        first = pl.multiple_of(chunk * CHUNK, CHUNK)
+
         @pl.when(place == 1)
         def _():
-            @pl.when(chunk == 0)
-            def _():
-                send_edges(right_ends, 0, early, first, CHUNK, send_far, recv_early.at[0], hub_q)
-
-            @pl.when(chunk > 0)
-            def _():
-                send_edges(right_ends, 0, early, first, CHUNK, send_right, recv_first.at[0, chunk])
-
             send_edges(left_ends, 0, early, first, CHUNK, send_left, recv_first.at[1, chunk])
 
     def send_right_late(group):
@@ -229,7 +274,7 @@
         for to_lane in range(zone):
             first = (quarter % 2 * zone + to_lane) * row_count + chunk * CHUNK
             rows = pl.ds(pl.multiple_of(first, CHUNK), CHUNK)
-            pass_on(left.at[pl.ds(0, early), rows, :], hub_q, recv_left.at[1, 0])
+            pass_on(left.at[pl.ds(shared, early - shared), rows, :], hub_q, recv_left.at[1, 0])
 
     def cross_early(chunk):
         await_part(right_rows(0, early, 0, zone * CHUNK), recv_early.at[chunk])
@@ -252,48 +297,88 @@
         climb_left(group - 1)
         return carry
 
-    def triangle(chan, count, group):
+    far_first = (1 - half) * group_rows * row_count
+    own_first = pl.multiple_of(quarter % 2 * zone * row_count, CHUNK)
+
+    j_half = group_rows * row_count
+    col_half = ka_n // 2
+
+    def multiply(chan, count, first, size, j_first, j_size):
+        j_rows = pl.ds(pl.multiple_of(j_first, 128), j_size)
+
+        def one_channel(at, carry):
+            tri[at, pl.ds(first, size), j_rows] = lax.dot_general(
+                left[at, pl.ds(first, size), :], right[at, j_rows, :], (((1,), (1,)), ((), ())),
+                preferred_element_type=jnp.float32,
+            ).astype(jnp.bfloat16)
+            return carry
+
+        lax.fori_loop(chan, chan + count, one_channel, 0)
+
+    def give_all(chan, count, base, spots, me, side, landed):
+        slot = back.at[pl.ds(member * share + chan, count)]
+
+        def part(to_spot, to_col):
+            first = (base - half * group_rows + to_spot) * row_count
+            return tri.at[
+                pl.ds(chan, count),
+                pl.ds(pl.multiple_of(first, CHUNK), row_count),
+                pl.ds(pl.multiple_of(to_col * col_count, 128), col_count),
+            ]
+
+        def give(step, carry):
+            to_spot = (me + step % spots) % spots
+            to_col = side * col_half + (col + step // spots) % col_half
+            pltpu.make_async_remote_copy(
+                src_ref=part(to_spot, to_col), dst_ref=slot, send_sem=send_tri, recv_sem=landed,
+                device_id=(base + to_spot, to_col), device_id_type=MESH,
+            ).start()
+            return carry
+
+        @pl.when(col // col_half == side)
+        def _():
+            pltpu.make_async_copy(part(me, col), slot, landed).start()
+
+        @pl.when(col // col_half != side)
+        def _():
+            give(0, 0)
+
+        lax.fori_loop(1, spots * col_half, give, 0)
+
+    def side_triangle(chan, count, side, landed):
+        multiply(chan, count, 0, group_rows * row_count, side * j_half, j_half)
+        give_all(chan, count, half * group_rows, group_rows, spot, side, landed)
+
+    def triangle(chan, count, group, landed):
         await_part(left_rows(chan, count, hub_q), recv_left.at[0, group])
         await_part(left_rows(chan, count, edge_q), recv_left.at[1, group])
-        await_part(right_rows(chan, count, 0, group_rows * row_count), recv_far.at[group])
-
-        def one_channel(at, carry):
-            tri[at] = lax.dot_general(
-                left[at], right[at], (((1,), (1,)), ((), ())), preferred_element_type=jnp.float32
-            ).astype(jnp.bfloat16)
-            return carry
-
-        lax.fori_loop(chan, chan + count, one_channel, 0)
-        slot = back.at[pl.ds(member * share + chan, count)]
-
-        def tri_part(to_spot, to_col):
-            return tri.at[
-                pl.ds(chan, count),
-                pl.ds(pl.multiple_of(to_spot * row_count, CHUNK), row_count),
-                pl.ds(pl.multiple_of(to_col * col_count, 128), col_count),
-            ]
-
-        def give(step, carry):
-            to_spot, to_col = (spot + step % group_rows) % group_rows, (col + step // group_rows) % ka_n
-            pltpu.make_async_remote_copy(
-                src_ref=tri_part(to_spot, to_col), dst_ref=slot,
-                send_sem=send_tri, recv_sem=recv_tri,
-                device_id=(half * group_rows + to_spot, to_col), device_id_type=MESH,
-            ).start()
-            return carry
-
-        lax.fori_loop(1, members, give, 0)
-        pltpu.make_async_copy(tri_part(spot, col), slot, recv_tri).start()
+        side_triangle(chan, count, half, landed)
+        await_part(right_rows(chan, count, far_first, group_rows * row_count), recv_far.at[group])
+        side_triangle(chan, count, 1 - half, landed)
+
+    def own_triangle():
+        for side in range(2):
+            multiply(0, shared, own_first, zone * row_count, side * j_half, j_half)
+            give_all(0, shared, quarter * zone, zone, lane, side, recv_tri.at[0])
 
     for small in smalls[2:]:
         small.wait()
-    make_chunk(0)
-    pl.semaphore_wait(barrier, rows_n * ka_n - 1)
-    send_early(0)
+    make_first()
+    pl.semaphore_wait(barrier, members - 1 + hubs * (1 - place))
+
+    @pl.when(place == 1)
+    def _():
+        send_edges(right_ends, 0, early, 0, CHUNK, send_far, recv_early.at[0], hub_q)
+        send_edges(right_ends, 0, shared, 0, CHUNK, send_right, recv_first.at[0, 0])
+
+    send_early_right(0)
+    make_first_left()
+    send_early_left(0)
 
     def rest(chunk, carry):
         make_chunk(chunk)
-        send_early(chunk)
+        send_early_right(chunk)
+        send_early_left(chunk)
 
         @pl.when(place == 1)
         def _():
@@ -336,9 +421,15 @@
                 cross_near(chunk)
         for group in range(late - ahead, late):
             send_left_late(group)
-
-    gain_col[...] = jnp.broadcast_to(out_gain_ref[...], (col_count, hidden)).T
-    bias_col[...] = jnp.broadcast_to(out_bias_ref[...], (col_count, hidden)).T
+        own_rows = hub_q * zone * row_count
+        await_part(right_rows(0, early, own_rows, zone * row_count), recv_own)
+        pass_on(right_rows(0, shared, own_rows, zone * row_count), edge_q, recv_down)
+
+    weights = w_out_ref[...].astype(jnp.float32)
+    gain_col = jnp.broadcast_to(out_gain_ref[...], (chans, hidden)).T
+    bias_col = jnp.broadcast_to(out_bias_ref[...], (chans, hidden)).T
+    w_scaled[...] = (weights * gain_col).astype(jnp.bfloat16)
+    bias_row[...] = jnp.sum(weights * bias_col, axis=0, keepdims=True)
 
     def gate_row(at, carry):
         gates[at] = sigmoid(
@@ -352,14 +443,22 @@
     def _():
         lax.fori_loop(2, late, climb, 0)
         climb_left(late - 1)
+        await_part(right_rows(0, shared, 0, zone * CHUNK), recv_first.at[0, 0])
+        await_part(right_rows(0, shared, 0, 3 * zone * row_count), recv_down)
+        own_triangle()
 
     @pl.when(inner)
     def _():
         for group in range(min(chunks, ahead), ahead + 1):
             cross_near(group)
         cross_edge(0)
-        await_part(right_rows(0, early, hub_q * zone * row_count, zone * row_count), recv_own)
-        triangle(0, early, 0)
+        await_part(left_rows(0, early, hub_q), recv_left.at[0, 0])
+        await_part(left_rows(shared, early - shared, edge_q), recv_left.at[1, 0])
+        await_part(right_rows(0, early, 0, group_rows * row_count), recv_far.at[0])
+        pass_on(right_rows(0, shared, far_first, group_rows * row_count), edge_q, recv_down)
+        own_triangle()
+        for side in range(2):
+            side_triangle(shared, early - shared, side, recv_tri.at[0])
 
         def stage(group, carry):
             @pl.when(group + ahead < late)
@@ -367,31 +466,50 @@
                 cross_near(group + ahead)
 
             cross_edge(group)
-            triangle(early + group - 1, 1, group)
+            triangle(early + group - 1, 1, group, recv_tri.at[0])
             return carry
 
         lax.fori_loop(1, late, stage, 0)
-        triangle(share - 1, 1, late)
-
-    pltpu.make_async_copy(back, back, recv_tri).wait()
+        triangle(share - 1, 1, late, recv_tri.at[1])
+
+    await_part(back.at[pl.ds(0, hidden - hubs)], recv_tri.at[0])
+    known = hidden - hubs
+
+    def by_member(chunk):
+        sums = back[:, chunk_rows(chunk), :].astype(jnp.float32)
+        return sums.reshape(hubs, share, CHUNK, col_count)
+
+    def gather_stats(chunk, carry):
+        rows = chunk_rows(chunk)
+        some = [back[at * share : at * share + share - 1, rows, :].astype(jnp.float32) for at in range(hubs)]
+        center = sum(jnp.sum(sums, axis=0) for sums in some) / known
+        mean_part[rows, :] = center
+        square_part[rows, :] = sum(jnp.sum((sums - center) * (sums - center), axis=0) for sums in some)
+        return carry
+
+    lax.fori_loop(0, chunks, gather_stats, 0)
+    await_part(back.at[pl.ds(0, hubs)], recv_tri.at[1])
 
     def finish(chunk, carry):
         first = pl.multiple_of(chunk * CHUNK, CHUNK)
-        sums = back[:, pl.ds(first, CHUNK), :].astype(jnp.float32)
-        center = jnp.mean(sums, axis=0, keepdims=True)
-        deviate = sums - center
-        spread = jnp.mean(deviate * deviate, axis=0, keepdims=True)
-        scaled = deviate * lax.rsqrt(spread + 1e-05)
-        planes[:hidden, :CHUNK, :] = scaled
+        sums = by_member(chunk)
+        last = sums[:, share - 1]
+        part = mean_part[chunk_rows(chunk), :]
+        center = (part * known + jnp.sum(last, axis=0)) / hidden
+        moved = part - center
+        left_over = last - center
+        squares = square_part[chunk_rows(chunk), :] + known * moved * moved
+        squares = squares + jnp.sum(left_over * left_over, axis=0)
+        scale = lax.rsqrt(squares / hidden + 1e-05)
+        planes[:hidden, :CHUNK, :] = ((sums - center) * scale).reshape(hidden, CHUNK, col_count)
 
         def one_row(local, inner_carry):
             at = first + local
-            chans_first = wide[pl.ds(local, hidden, stride=PITCH), :]
-            tri_normed = (chans_first * gain_col[...] + bias_col[...]).astype(jnp.bfloat16)
+            tri_normed = wide[pl.ds(local, hidden, stride=PITCH), :].astype(jnp.bfloat16)
             projected = lax.dot_general(
-                tri_normed, w_out_ref[...], (((0,), (0,)), ((), ())), preferred_element_type=jnp.float32
+                tri_normed, w_scaled[...], (((0,), (0,)), ((), ())), preferred_element_type=jnp.float32
             )
-            out_ref[at] = (gates[at] * projected).astype(jnp.bfloat16)
+            out_ref[at] = (gates[at] * (projected + bias_row[...])).astype(jnp.bfloat16)
             return inner_carry
 
         lax.fori_loop(0, CHUNK, one_row, 0, unroll=FINISH_UNROLL)
@@ -411,19 +529,29 @@
     sent_all(0, (hubs - 1) * late, row_count, send_right)
     sent_all(CHUNK, (hubs - 1) * early, row_count - CHUNK, send_right)
 
+    @pl.when(place == 1)
+    def _():
+        sent_all(0, (hubs - 1) * shared, CHUNK, send_right)
+
     @pl.when(inner)
     def _():
         sent_all(0, (hubs - 1) * early, CHUNK, send_right)
 
-    passed = right.at[:, pl.ds(0, group_rows * row_count), :]
-    await_part(passed, send_far)
+    def given_all(count, spots):
+        if spots > 1:
+            await_part(tri.at[pl.ds(0, count), pl.ds(0, (spots - 1) * row_count), :], send_tri)
+        await_part(tri.at[pl.ds(0, count), pl.ds(0, row_count), pl.ds(0, (ka_n - 1) * col_count)], send_tri)
+
+    plane = zone * row_count
+    await_part(right.at[:, pl.ds(0, plane), :], send_far)
+    await_part(right.at[pl.ds(0, share - shared), pl.ds(0, plane), :], send_far)
+    given_all(shared, zone)
 
     @pl.when(inner)
     def _():
-        most = tri.at[:, pl.ds(0, (group_rows - 1) * row_count), :]
-        pltpu.make_async_copy(most, most, send_tri).wait()
-        more = tri.at[:, pl.ds(0, row_count), pl.ds(0, (ka_n - 1) * col_count)]
-        pltpu.make_async_copy(more, more, send_tri).wait()
+        await_part(right.at[pl.ds(0, shared), pl.ds(0, 2 * plane), :], send_far)
+        await_part(right.at[pl.ds(0, shared), pl.ds(0, 2 * plane), :], send_far)
+        given_all(share - shared, group_rows)
 
 
 def fused(rows_n, ka_n, args):
@@ -460,8 +588,10 @@
             pltpu.VMEM((share, rows_n // 2 * row_count, ka_n * col_count), half),
             pltpu.VMEM((hidden, row_count, col_count), half),
             pltpu.VMEM((4 * hidden, chans), half),
-            pltpu.VMEM((hidden, col_count), jnp.float32),
-            pltpu.VMEM((hidden, col_count), jnp.float32),
+            pltpu.VMEM((hidden, chans), half),
+            pltpu.VMEM((1, chans), jnp.float32),
+            pltpu.VMEM((row_count, col_count), jnp.float32),
+            pltpu.VMEM((row_count, col_count), jnp.float32),
             pltpu.SemaphoreType.DMA((9,)),
             pltpu.SemaphoreType.DMA((chunks,)),
             pltpu.SemaphoreType.DMA,
@@ -469,9 +599,10 @@
             pltpu.SemaphoreType.DMA((2, chunks)),
             pltpu.SemaphoreType.DMA((chunks,)),
             pltpu.SemaphoreType.DMA,
+            pltpu.SemaphoreType.DMA,
             pltpu.SemaphoreType.DMA((2, late)),
             pltpu.SemaphoreType.DMA((1 + late,)),
-            pltpu.SemaphoreType.DMA,
+            pltpu.SemaphoreType.DMA((2,)),
             pltpu.SemaphoreType.DMA,
             pltpu.SemaphoreType.DMA,
             pltpu.SemaphoreType.DMA,
@@ -522,7 +653,7 @@
     hidden = args[-1].shape[0]
     hubs = rows_n // 4 * ka_n
     aligned = row_count % CHUNK == 0 and col_count % 128 == 0 and chans % 128 == 0 and hidden % 128 == 0
-    if aligned and rows_n % 4 == 0 and hidden % hubs == 0 and col_count == hidden:
+    if aligned and rows_n % 4 == 0 and ka_n % 2 == 0 and hidden % hubs == 0 and col_count == hidden:
         if hidden // hubs - EARLY > AHEAD and row_count > CHUNK:
             return fused(rows_n, ka_n, args)
     return plain(args)

time: 111 us -> 105 us (0.946)
  Pallas kernels: 109 us -> 104 us
    pallas_call x1, Pallas kernels: 109 us -> 104 us  [fused(): pl.pallas_call(functools.partial(kernel, rows_n, ka_n, EARLY), out_shape=...]
where the time goes in v3:
time: 105 us
  Pallas kernels  104 us (99%)
  local copies, waits for them, and re-layouts  1.32 us (1%)
    pallas_call x1, Pallas kernels, fused(): pl.pallas_call(functools.partial(kernel, rows_n, ka_n, EARLY), out_shape=...  104 us

profile of v3, /device:TPU:0, one launch (start us, length us, event | category | flops | bytes accessed | tf_op | source)
XLA Modules:
  0.0 105.2 jit_solution(2611115926731696768)
XLA Ops:
  0.0 103.9 %shard_map.100 = bf16[64,128,128]{2,1,0:T(8,128)(2,1)S(1)} custom-call(bf16[64,128,128]{2,1,0:T(8,128)(2,1)} %pair_hbm.1, s32[64,128]{1,0:T(8,128)} %mask_hbm.1, f32[1,128]{1,0:T(1,128)} %bitcast.4, f32[1,128]{1,0:T(1,128)} %bitcast.5, bf16[128,256]{1,0:T(8,128)(2,1)} %w_proj_hbm.1, bf16[128,256]{1,0:T(8,128)(2,1)} %w_gate_hbm.1, ...), custom_call_target="tpu_custom_call" | custom-call | tf_op jit(solution)/shard_map/pallas_call | solution.py:565
  103.9 1.3 %copy.12 = bf16[64,128,128]{2,1,0:T(8,128)(2,1)} copy(bf16[64,128,128]{2,1,0:T(8,128)(2,1)S(1)} %shard_map.100) | data formatting | bytes 4194304

commit v4 on v3

--- a/solution.py
+++ b/solution.py
@@ -179,7 +179,7 @@
             make_side(at, at, normalise(at), 0, hidden)
             return carry
 
-        lax.fori_loop(0, CHUNK, right_row, 0, unroll=MAKE_UNROLL)
+        lax.fori_loop(0, CHUNK, right_row, 0, unroll=CHUNK)
         round_side(0, hidden, hidden)
 
     def make_first_left():
@@ -208,7 +208,7 @@
 
         @pl.when(inner)
         def _():
-            send_edges(right_ends, 0, early, first, CHUNK, send_far, recv_far.at[0], far_q)
+            send_edges(right_ends, 0, early, first, CHUNK, send_far, recv_far.at[0, 0], far_q)
 
         @pl.when((place == 1) & (chunk > 0))
         def _():
@@ -278,13 +278,13 @@
 
     def cross_early(chunk):
         await_part(right_rows(0, early, 0, zone * CHUNK), recv_early.at[chunk])
-        pass_early(edge_q, chunk, far_q, recv_far.at[0])
+        pass_early(edge_q, chunk, far_q, recv_far.at[1, 0])
 
     def cross_near(group):
-        pass_late(hub_q, group, far_q, recv_right.at[0, group], recv_far.at[1 + group])
+        pass_late(hub_q, group, far_q, recv_right.at[0, group], recv_far.at[0, 1 + group])
 
     def cross_edge(group):
-        pass_late(edge_q, group, far_q, recv_right.at[1, group], recv_far.at[1 + group])
+        pass_late(edge_q, group, far_q, recv_right.at[1, group], recv_far.at[1, 1 + group])
 
     def climb_right(group):
         pass_late(edge_q, group, hub_q, recv_right.at[0, group], recv_right.at[1, group])
@@ -300,8 +300,8 @@
     far_first = (1 - half) * group_rows * row_count
     own_first = pl.multiple_of(quarter % 2 * zone * row_count, CHUNK)
 
-    j_half = group_rows * row_count
-    col_half = ka_n // 2
+    j_block = zone * row_count
+    col_block = ka_n // 4
 
     def multiply(chan, count, first, size, j_first, j_size):
         j_rows = pl.ds(pl.multiple_of(j_first, 128), j_size)
@@ -315,7 +315,7 @@
 
         lax.fori_loop(chan, chan + count, one_channel, 0)
 
-    def give_all(chan, count, base, spots, me, side, landed):
+    def give_all(chan, count, base, spots, me, col_first, col_size, landed):
         slot = back.at[pl.ds(member * share + chan, count)]
 
         def part(to_spot, to_col):
@@ -328,38 +328,68 @@
 
         def give(step, carry):
             to_spot = (me + step % spots) % spots
-            to_col = side * col_half + (col + step // spots) % col_half
+            to_col = col_first + (col + step // spots) % col_size
             pltpu.make_async_remote_copy(
                 src_ref=part(to_spot, to_col), dst_ref=slot, send_sem=send_tri, recv_sem=landed,
                 device_id=(base + to_spot, to_col), device_id_type=MESH,
             ).start()
             return carry
 
-        @pl.when(col // col_half == side)
+        mine = (col >= col_first) & (col < col_first + col_size)
+
+        @pl.when(mine)
         def _():
             pltpu.make_async_copy(part(me, col), slot, landed).start()
 
-        @pl.when(col // col_half != side)
+        @pl.when(jnp.logical_not(mine))
         def _():
             give(0, 0)
 
-        lax.fori_loop(1, spots * col_half, give, 0)
-
-    def side_triangle(chan, count, side, landed):
-        multiply(chan, count, 0, group_rows * row_count, side * j_half, j_half)
-        give_all(chan, count, half * group_rows, group_rows, spot, side, landed)
-
-    def triangle(chan, count, group, landed):
+        lax.fori_loop(1, spots * col_size, give, 0)
+
+    def block(chan, count, from_q, quarters, landed):
+        multiply(chan, count, 0, group_rows * row_count, from_q * j_block, quarters * j_block)
+        give_all(
+            chan, count, half * group_rows, group_rows, spot, from_q * col_block, quarters * col_block, landed
+        )
+
+    def near_block(chan, count, group, landed):
         await_part(left_rows(chan, count, hub_q), recv_left.at[0, group])
         await_part(left_rows(chan, count, edge_q), recv_left.at[1, group])
-        side_triangle(chan, count, half, landed)
-        await_part(right_rows(chan, count, far_first, group_rows * row_count), recv_far.at[group])
-        side_triangle(chan, count, 1 - half, landed)
+        block(chan, count, 2 * half, 2, landed)
+
+    def far_block(chan, count, group, landed):
+        for where in range(2):
+            far_part(where, chan, count, group, landed)
+
+    def far_part(where, chan, count, group, landed):
+        from_q = far_q if where == 0 else 3 * (1 - half)
+        part = right_rows(chan, count, from_q * zone * row_count, zone * row_count)
+        await_part(part, recv_far.at[where, group])
+        block(chan, count, from_q, 1, landed)
 
     def own_triangle():
-        for side in range(2):
-            multiply(0, shared, own_first, zone * row_count, side * j_half, j_half)
-            give_all(0, shared, quarter * zone, zone, lane, side, recv_tri.at[0])
+        multiply(0, shared, own_first, zone * row_count, 0, rows_n * row_count)
+        give_all(0, shared, quarter * zone, zone, lane, 0, ka_n, recv_tri.at[0])
+
+    known = hidden - hubs
+
+    def gather_stats():
+        await_part(back.at[pl.ds(0, known)], recv_tri.at[0])
+
+        def one_chunk(chunk, carry):
+            rows = chunk_rows(chunk)
+            some = [
+                back[at * share : at * share + share - 1, rows, :].astype(jnp.float32) for at in range(hubs)
+            ]
+            center = sum(jnp.sum(sums, axis=0) for sums in some) / known
+            mean_part[rows, :] = center
+            square_part[rows, :] = sum(
+                jnp.sum((sums - center) * (sums - center), axis=0) for sums in some
+            )
+            return carry
+
+        lax.fori_loop(0, chunks, one_chunk, 0)
 
     for small in smalls[2:]:
         small.wait()
@@ -454,52 +484,52 @@
         cross_edge(0)
         await_part(left_rows(0, early, hub_q), recv_left.at[0, 0])
         await_part(left_rows(shared, early - shared, edge_q), recv_left.at[1, 0])
-        await_part(right_rows(0, early, 0, group_rows * row_count), recv_far.at[0])
+        for where, from_q in ((0, far_q), (1, 3 * (1 - half))):
+            await_part(right_rows(0, early, from_q * zone * row_count, zone * row_count), recv_far.at[where, 0])
         pass_on(right_rows(0, shared, far_first, group_rows * row_count), edge_q, recv_down)
         own_triangle()
-        for side in range(2):
-            side_triangle(shared, early - shared, side, recv_tri.at[0])
+        block(shared, early - shared, 0, 4, recv_tri.at[0])
+
+        def near_upto(group):
+            return ahead + 1 + (late - ahead - 1) * group // (late - 1)
+
+        def near_one(group, carry):
+            cross_near(group)
+            return carry
 
         def stage(group, carry):
-            @pl.when(group + ahead < late)
-            def _():
-                cross_near(group + ahead)
-
+            lax.fori_loop(near_upto(group - 1), near_upto(group), near_one, 0)
             cross_edge(group)
-            triangle(early + group - 1, 1, group, recv_tri.at[0])
+            near_block(early + group - 1, 1, group, recv_tri.at[0])
+            far_block(early + group - 1, 1, group, recv_tri.at[0])
             return carry
 
         lax.fori_loop(1, late, stage, 0)
-        triangle(share - 1, 1, late, recv_tri.at[1])
-
-    await_part(back.at[pl.ds(0, hidden - hubs)], recv_tri.at[0])
-    known = hidden - hubs
+        near_block(share - 1, 1, late, recv_tri.at[1])
+        far_part(0, share - 1, 1, late, recv_tri.at[1])
+        gather_stats()
+        far_part(1, share - 1, 1, late, recv_tri.at[1])
+
+    @pl.when(place == 1)
+    def _():
+        gather_stats()
+
+    await_part(back.at[pl.ds(0, hubs)], recv_tri.at[1])
 
     def by_member(chunk):
         sums = back[:, chunk_rows(chunk), :].astype(jnp.float32)
         return sums.reshape(hubs, share, CHUNK, col_count)
 
-    def gather_stats(chunk, carry):
-        rows = chunk_rows(chunk)
-        some = [back[at * share : at * share + share - 1, rows, :].astype(jnp.float32) for at in range(hubs)]
-        center = sum(jnp.sum(sums, axis=0) for sums in some) / known
-        mean_part[rows, :] = center
-        square_part[rows, :] = sum(jnp.sum((sums - center) * (sums - center), axis=0) for sums in some)
-        return carry
-
-    lax.fori_loop(0, chunks, gather_stats, 0)
-    await_part(back.at[pl.ds(0, hubs)], recv_tri.at[1])
-
     def finish(chunk, carry):
         first = pl.multiple_of(chunk * CHUNK, CHUNK)
         sums = by_member(chunk)
-        last = sums[:, share - 1]
+        last = sums[:, share - 1 :]
         part = mean_part[chunk_rows(chunk), :]
-        center = (part * known + jnp.sum(last, axis=0)) / hidden
+        center = (part * known + jnp.sum(last, axis=(0, 1))) / hidden
         moved = part - center
         left_over = last - center
         squares = square_part[chunk_rows(chunk), :] + known * moved * moved
-        squares = squares + jnp.sum(left_over * left_over, axis=0)
+        squares = squares + jnp.sum(left_over * left_over, axis=(0, 1))
         scale = lax.rsqrt(squares / hidden + 1e-05)
         planes[:hidden, :CHUNK, :] = ((sums - center) * scale).reshape(hidden, CHUNK, col_count)
 
@@ -601,7 +631,7 @@
             pltpu.SemaphoreType.DMA,
             pltpu.SemaphoreType.DMA,
             pltpu.SemaphoreType.DMA((2, late)),
-            pltpu.SemaphoreType.DMA((1 + late,)),
+            pltpu.SemaphoreType.DMA((2, 1 + late)),
             pltpu.SemaphoreType.DMA((2,)),
             pltpu.SemaphoreType.DMA,
             pltpu.SemaphoreType.DMA,
@@ -653,7 +683,7 @@
     hidden = args[-1].shape[0]
     hubs = rows_n // 4 * ka_n
     aligned = row_count % CHUNK == 0 and col_count % 128 == 0 and chans % 128 == 0 and hidden % 128 == 0
-    if aligned and rows_n % 4 == 0 and ka_n % 2 == 0 and hidden % hubs == 0 and col_count == hidden:
+    if aligned and rows_n % 4 == 0 and ka_n % 4 == 0 and hidden % hubs == 0 and col_count == hidden:
         if hidden // hubs - EARLY > AHEAD and row_count > CHUNK:
             return fused(rows_n, ka_n, args)
     return plain(args)

time: 105 us -> 105 us (level); the launches traced: 105 us -> 104 us
  Pallas kernels: 104 us -> 102 us
    pallas_call x1, Pallas kernels: 104 us -> 102 us  [fused(): pl.pallas_call(functools.partial(kernel, rows_n, ka_n, EARLY), out_shape=...]
where the time goes in v4:
time: 105 us; the launch traced here: 104 us
  Pallas kernels  102 us (97%)
  local copies, waits for them, and re-layouts  1.32 us (1%)
    pallas_call x1, Pallas kernels, fused(): pl.pallas_call(functools.partial(kernel, rows_n, ka_n, EARLY), out_shape=...  102 us

profile of v4, /device:TPU:0, one launch (start us, length us, event | category | flops | bytes accessed | tf_op | source)
XLA Modules:
  0.0 103.6 jit_solution(14482610933687488194)
XLA Ops:
  0.0 102.2 %shard_map.100 = bf16[64,128,128]{2,1,0:T(8,128)(2,1)S(1)} custom-call(bf16[64,128,128]{2,1,0:T(8,128)(2,1)} %pair_hbm.1, s32[64,128]{1,0:T(8,128)} %mask_hbm.1, f32[1,128]{1,0:T(1,128)} %bitcast.4, f32[1,128]{1,0:T(1,128)} %bitcast.5, bf16[128,256]{1,0:T(8,128)(2,1)} %w_proj_hbm.1, bf16[128,256]{1,0:T(8,128)(2,1)} %w_gate_hbm.1, ...), custom_call_target="tpu_custom_call" | custom-call | tf_op jit(solution)/shard_map/pallas_call | solution.py:595
  102.2 1.3 %copy.12 = bf16[64,128,128]{2,1,0:T(8,128)(2,1)} copy(bf16[64,128,128]{2,1,0:T(8,128)(2,1)S(1)} %shard_map.100) | data formatting | bytes 4194304

commit v5 on v4

--- a/solution.py
+++ b/solution.py
@@ -33,12 +33,12 @@
     rows_n, ka_n, early,
     pair_hbm, mask_hbm, ln_gain_hbm, ln_bias_hbm, w_proj_hbm, w_gate_hbm, w_out_gate_hbm,
     out_gain_hbm, out_bias_hbm, w_out_hbm,
-    out_hbm,
+    out_ref,
     mask_ref, ln_gain_ref, ln_bias_ref, w_proj_ref, w_gate_ref, w_out_gate_ref,
     out_gain_ref, out_bias_ref, w_out_ref,
-    pair_ref, out_ref, edges, wide, normed, gates, left, right, tri, back, w_cat, w_scaled, bias_row,
+    pair_ref, edges, wide, normed, gates, left, right, tri, back, w_cat, w_scaled, bias_row,
     mean_part, square_part,
-    small_sem, load_sem, store_sem, recv_left, recv_first, recv_early, recv_own, recv_down, recv_right, recv_far, recv_tri,
+    small_sem, load_sem, recv_left, recv_first, recv_early, recv_own, recv_down, recv_right, recv_far, recv_tri,
     send_left, send_right, send_far, send_tri,
 ):
     row = lax.axis_index("rows")
@@ -420,17 +420,22 @@
 
     @pl.when(place == 1)
     def _():
+        send_right_late(0)
+        send_both(0, 1)
+        send_both(1, 1)
         climb_early(chunks - 1)
-        send_right_late(0)
+        send_both(2, 1)
+        climb_right(0)
+        send_both(3, 1)
+        climb(1, 0)
 
         def both(group, carry):
             send_both(group, 1)
             return carry
 
-        lax.fori_loop(0, late - 1, both, 0)
+        lax.fori_loop(4, late - 1, both, 0)
         send_left_late(late - 1)
-        climb_right(0)
-        climb(1, 0)
+        climb(2, 0)
 
     @pl.when(inner)
     def _():
@@ -471,7 +476,7 @@
 
     @pl.when(place == 1)
     def _():
-        lax.fori_loop(2, late, climb, 0)
+        lax.fori_loop(3, late, climb, 0)
         climb_left(late - 1)
         await_part(right_rows(0, shared, 0, zone * CHUNK), recv_first.at[0, 0])
         await_part(right_rows(0, shared, 0, 3 * zone * row_count), recv_down)
@@ -520,8 +525,7 @@
         sums = back[:, chunk_rows(chunk), :].astype(jnp.float32)
         return sums.reshape(hubs, share, CHUNK, col_count)
 
-    def finish(chunk, carry):
-        first = pl.multiple_of(chunk * CHUNK, CHUNK)
+    def scale_chunk(chunk, first_plane):
         sums = by_member(chunk)
         last = sums[:, share - 1 :]
         part = mean_part[chunk_rows(chunk), :]
@@ -531,11 +535,12 @@
         squares = square_part[chunk_rows(chunk), :] + known * moved * moved
         squares = squares + jnp.sum(left_over * left_over, axis=(0, 1))
         scale = lax.rsqrt(squares / hidden + 1e-05)
-        planes[:hidden, :CHUNK, :] = ((sums - center) * scale).reshape(hidden, CHUNK, col_count)
-
+        planes[first_plane : first_plane + hidden, :CHUNK, :] = ((sums - center) * scale).reshape(hidden, CHUNK, col_count)
+
+    def project_chunk(chunk, first_plane):
         def one_row(local, inner_carry):
-            at = first + local
-            tri_normed = wide[pl.ds(local, hidden, stride=PITCH), :].astype(jnp.bfloat16)
+            at = chunk * CHUNK + local
+            tri_normed = wide[pl.ds(local + first_plane * PITCH, hidden, stride=PITCH), :].astype(jnp.bfloat16)
             projected = lax.dot_general(
                 tri_normed, w_scaled[...], (((0,), (0,)), ((), ())), preferred_element_type=jnp.float32
             )
@@ -543,13 +548,13 @@
             return inner_carry
 
         lax.fori_loop(0, CHUNK, one_row, 0, unroll=FINISH_UNROLL)
-        pltpu.make_async_copy(
-            out_ref.at[chunk_rows(chunk)], out_hbm.at[chunk_rows(chunk)], store_sem
-        ).start()
-        return carry
-
-    lax.fori_loop(0, chunks, finish, 0)
-    pltpu.make_async_copy(out_ref, out_hbm, store_sem).wait()
+
+    scale_chunk(0, 0)
+
+    for chunk in range(chunks):
+        if chunk + 1 < chunks:
+            scale_chunk(chunk + 1, (chunk + 1) % 2 * hidden)
+        project_chunk(chunk, chunk % 2 * hidden)
 
     def sent_all(first, count, rows, sem):
         part = edges.at[pl.ds(0, count), pl.ds(first, rows), :]
@@ -596,7 +601,7 @@
         functools.partial(kernel, rows_n, ka_n, EARLY),
         out_shape=jax.ShapeDtypeStruct(pair_repr.shape, half),
         in_specs=[pl.BlockSpec(memory_space=pltpu.HBM)] * 10,
-        out_specs=pl.BlockSpec(memory_space=pl.ANY),
+        out_specs=pl.BlockSpec(memory_space=pltpu.VMEM),
         scratch_shapes=[
             pltpu.VMEM((row_count, col_count), jnp.int32),
             pltpu.VMEM((1, chans), jnp.float32),
@@ -607,7 +612,6 @@
             pltpu.VMEM((1, hidden), jnp.float32),
             pltpu.VMEM((1, hidden), jnp.float32),
             pltpu.VMEM((hidden, chans), half),
-            pltpu.VMEM((row_count, col_count, chans), half),
             pltpu.VMEM((row_count, col_count, chans), half),
             pltpu.VMEM((2 * hidden, row_count, col_count), half),
             pltpu.VMEM((2 * hidden * PITCH, col_count), jnp.float32),
@@ -624,7 +628,6 @@
             pltpu.VMEM((row_count, col_count), jnp.float32),
             pltpu.SemaphoreType.DMA((9,)),
             pltpu.SemaphoreType.DMA((chunks,)),
-            pltpu.SemaphoreType.DMA,
             pltpu.SemaphoreType.DMA((2, 1 + late)),
             pltpu.SemaphoreType.DMA((2, chunks)),
             pltpu.SemaphoreType.DMA((chunks,)),
@@ -684,7 +687,7 @@
     hubs = rows_n // 4 * ka_n
     aligned = row_count % CHUNK == 0 and col_count % 128 == 0 and chans % 128 == 0 and hidden % 128 == 0
     if aligned and rows_n % 4 == 0 and ka_n % 4 == 0 and hidden % hubs == 0 and col_count == hidden:
-        if hidden // hubs - EARLY > AHEAD and row_count > CHUNK:
+        if hidden // hubs - EARLY > max(AHEAD, 5) and row_count > CHUNK:
             return fused(rows_n, ka_n, args)
     return plain(args)
 

time: 105 us -> 104 us (level)
  no operation moved by 1% of the time
where the time goes in v5:
time: 104 us; the launch traced here: 103 us
  Pallas kernels  102 us (98%)
  local copies, waits for them, and re-layouts  1.32 us (1%)
    pallas_call x1, Pallas kernels, fused(): pl.pallas_call(functools.partial(kernel, rows_n, ka_n, EARLY), out_shape=...  102 us

profile of v5, /device:TPU:0, one launch (start us, length us, event | category | flops | bytes accessed | tf_op | source)
XLA Modules:
  0.0 103.0 jit_solution(6746639007982811558)
XLA Ops:
  0.0 101.7 %shard_map.100 = bf16[64,128,128]{2,1,0:T(8,128)(2,1)S(1)} custom-call(bf16[64,128,128]{2,1,0:T(8,128)(2,1)} %pair_hbm.1, s32[64,128]{1,0:T(8,128)} %mask_hbm.1, f32[1,128]{1,0:T(1,128)} %bitcast.4, f32[1,128]{1,0:T(1,128)} %bitcast.5, bf16[128,256]{1,0:T(8,128)(2,1)} %w_proj_hbm.1, bf16[128,256]{1,0:T(8,128)(2,1)} %w_gate_hbm.1, ...), custom_call_target="tpu_custom_call" | custom-call | tf_op jit(solution)/shard_map/pallas_call | solution.py:600
  101.7 1.3 %copy.12 = bf16[64,128,128]{2,1,0:T(8,128)(2,1)} copy(bf16[64,128,128]{2,1,0:T(8,128)(2,1)S(1)} %shard_map.100) | data formatting | bytes 4194304

commit v6 on v5

--- a/solution.py
+++ b/solution.py
@@ -36,7 +36,7 @@
     out_ref,
     mask_ref, ln_gain_ref, ln_bias_ref, w_proj_ref, w_gate_ref, w_out_gate_ref,
     out_gain_ref, out_bias_ref, w_out_ref,
-    pair_ref, edges, wide, normed, gates, left, right, tri, back, w_cat, w_scaled, bias_row,
+    pair_ref, edges, wide, normed, gates, left, right, tri, back, w_cat, w_scaled, bias_row, w_tail, acc,
     mean_part, square_part,
     small_sem, load_sem, recv_left, recv_first, recv_early, recv_own, recv_down, recv_right, recv_far, recv_tri,
     send_left, send_right, send_far, send_tri,
@@ -466,6 +466,21 @@
     w_scaled[...] = (weights * gain_col).astype(jnp.bfloat16)
     bias_row[...] = jnp.sum(weights * bias_col, axis=0, keepdims=True)
 
+    def parts_of(values):
+        high = values.astype(jnp.bfloat16).astype(jnp.float32)
+        middle = (values - high).astype(jnp.bfloat16).astype(jnp.float32)
+        return high, middle, values - high - middle
+
+    rounded = w_scaled[...].astype(jnp.float32)
+    high, middle, low = parts_of(-jnp.sum(rounded, axis=0, keepdims=True))
+    none, one = jnp.zeros_like(high), jnp.ones_like(high)
+    late_rows = [rounded[at * share + share - 1 : at * share + share] for at in range(hubs)]
+    rows_plain = late_rows + [high, middle, low, high, middle, high, none, none]
+    rows_scale = [none] * (hubs + 6) + [one, one]
+    w_tail[...] = jnp.concatenate(
+        [jnp.concatenate(rows_plain, axis=0), jnp.concatenate(rows_scale, axis=0)], axis=1
+    ).astype(jnp.bfloat16)
+
     def gate_row(at, carry):
         gates[at] = sigmoid(
             jnp.dot(normed[at], w_out_gate_ref[...], preferred_element_type=jnp.float32)
@@ -519,42 +534,61 @@
     def _():
         gather_stats()
 
+    def lay_known(chunk, base):
+        for at in range(hubs):
+            first, size = at * share, share - 1
+            planes[base + first : base + first + size, :CHUNK, :] = (
+                back[first : first + size, chunk_rows(chunk), :].astype(jnp.float32)
+            )
+            planes[base + first + size, :CHUNK, :] = jnp.zeros((CHUNK, col_count), jnp.float32)
+
+    def project_known(chunk, base):
+        def one_row(local, carry):
+            sums = wide[pl.ds(local + base * PITCH, hidden, stride=PITCH), :].astype(jnp.bfloat16)
+            acc[chunk * CHUNK + local] = lax.dot_general(
+                sums, w_scaled[...], (((0,), (0,)), ((), ())), preferred_element_type=jnp.float32
+            )
+            return carry
+
+        lax.fori_loop(0, CHUNK, one_row, 0, unroll=FINISH_UNROLL)
+
+    def lay_last(chunk, base):
+        rows = chunk_rows(chunk)
+        last = [back[at * share + share - 1, rows, :].astype(jnp.float32) for at in range(hubs)]
+        part = mean_part[rows, :]
+        center = (part * known + sum(last)) / hidden
+        moved = part - center
+        squares = square_part[rows, :] + known * moved * moved
+        squares = squares + sum((sums - center) * (sums - center) for sums in last)
+        high, middle, low = parts_of(center)
+        scale, scale_rest, _ = parts_of(lax.rsqrt(squares / hidden + 1e-05))
+        stack = last + [high, high, high, middle, middle, low, scale, scale_rest]
+        for at, plane in enumerate(stack):
+            planes[base + at, :CHUNK, :] = plane
+
+    def project_last(chunk, base):
+        def one_row(local, carry):
+            at = chunk * CHUNK + local
+            stack = wide[pl.ds(local + base * PITCH, hubs + 8, stride=PITCH), :].astype(jnp.bfloat16)
+            tail = lax.dot_general(
+                stack, w_tail[...], (((0,), (0,)), ((), ())), preferred_element_type=jnp.float32
+            )
+            projected = (acc[at] + tail[:, :chans]) * tail[:, chans:] + bias_row[...]
+            out_ref[at] = (gates[at] * projected).astype(jnp.bfloat16)
+            return carry
+
+        lax.fori_loop(0, CHUNK, one_row, 0, unroll=FINISH_UNROLL)
+
+    def in_turns(lay, project):
+        lay(0, 0)
+        for chunk in range(chunks):
+            if chunk + 1 < chunks:
+                lay(chunk + 1, (chunk + 1) % 2 * hidden)
+            project(chunk, chunk % 2 * hidden)
+
+    in_turns(lay_known, project_known)
     await_part(back.at[pl.ds(0, hubs)], recv_tri.at[1])
-
-    def by_member(chunk):
-        sums = back[:, chunk_rows(chunk), :].astype(jnp.float32)
-        return sums.reshape(hubs, share, CHUNK, col_count)
-
-    def scale_chunk(chunk, first_plane):
-        sums = by_member(chunk)
-        last = sums[:, share - 1 :]
-        part = mean_part[chunk_rows(chunk), :]
-        center = (part * known + jnp.sum(last, axis=(0, 1))) / hidden
-        moved = part - center
-        left_over = last - center
-        squares = square_part[chunk_rows(chunk), :] + known * moved * moved
-        squares = squares + jnp.sum(left_over * left_over, axis=(0, 1))
-        scale = lax.rsqrt(squares / hidden + 1e-05)
-        planes[first_plane : first_plane + hidden, :CHUNK, :] = ((sums - center) * scale).reshape(hidden, CHUNK, col_count)
-
-    def project_chunk(chunk, first_plane):
-        def one_row(local, inner_carry):
-            at = chunk * CHUNK + local
-            tri_normed = wide[pl.ds(local + first_plane * PITCH, hidden, stride=PITCH), :].astype(jnp.bfloat16)
-            projected = lax.dot_general(
-                tri_normed, w_scaled[...], (((0,), (0,)), ((), ())), preferred_element_type=jnp.float32
-            )
-            out_ref[at] = (gates[at] * (projected + bias_row[...])).astype(jnp.bfloat16)
-            return inner_carry
-
-        lax.fori_loop(0, CHUNK, one_row, 0, unroll=FINISH_UNROLL)
-
-    scale_chunk(0, 0)
-
-    for chunk in range(chunks):
-        if chunk + 1 < chunks:
-            scale_chunk(chunk + 1, (chunk + 1) % 2 * hidden)
-        project_chunk(chunk, chunk % 2 * hidden)
+    in_turns(lay_last, project_last)
 
     def sent_all(first, count, rows, sem):
         part = edges.at[pl.ds(0, count), pl.ds(first, rows), :]
@@ -624,6 +658,8 @@
             pltpu.VMEM((4 * hidden, chans), half),
             pltpu.VMEM((hidden, chans), half),
             pltpu.VMEM((1, chans), jnp.float32),
+            pltpu.VMEM((hidden // share + 8, 2 * chans), half),
+            pltpu.VMEM((row_count, col_count, chans), jnp.float32),
             pltpu.VMEM((row_count, col_count), jnp.float32),
             pltpu.VMEM((row_count, col_count), jnp.float32),
             pltpu.SemaphoreType.DMA((9,)),

time: 104 us -> 104 us (level)
  no operation moved by 1% of the time
where the time goes in v6:
time: 104 us; the launch traced here: 102 us
  Pallas kernels  101 us (97%)
  local copies, waits for them, and re-layouts  1.32 us (1%)
    pallas_call x1, Pallas kernels, fused(): pl.pallas_call(functools.partial(kernel, rows_n, ka_n, EARLY), out_shape=...  101 us

profile of v6, /device:TPU:0, one launch (start us, length us, event | category | flops | bytes accessed | tf_op | source)
XLA Modules:
  0.0 102.5 jit_solution(8287146608379050425)
XLA Ops:
  0.0 101.1 %shard_map.100 = bf16[64,128,128]{2,1,0:T(8,128)(2,1)S(1)} custom-call(bf16[64,128,128]{2,1,0:T(8,128)(2,1)} %pair_hbm.1, s32[64,128]{1,0:T(8,128)} %mask_hbm.1, f32[1,128]{1,0:T(1,128)} %bitcast.4, f32[1,128]{1,0:T(1,128)} %bitcast.5, bf16[128,256]{1,0:T(8,128)(2,1)} %w_proj_hbm.1, bf16[128,256]{1,0:T(8,128)(2,1)} %w_gate_hbm.1, ...), custom_call_target="tpu_custom_call" | custom-call | tf_op jit(solution)/shard_map/pallas_call | solution.py:634
  101.1 1.3 %copy.12 = bf16[64,128,128]{2,1,0:T(8,128)(2,1)} copy(bf16[64,128,128]{2,1,0:T(8,128)(2,1)S(1)} %shard_map.100) | data formatting | bytes 4194304

commit v7 on v6

--- a/solution.py
+++ b/solution.py
@@ -196,8 +196,14 @@
         def one_row(local, carry):
             at = chunk * CHUNK + local
             plain = normalise(at)
-            make_side(at, local, plain, 0, hidden)
-            make_side(at, local, plain, 2 * hidden, 0)
+            both = lax.dot_general(
+                w_cat[...], plain, (((1,), (1,)), ((), ())), preferred_element_type=jnp.float32
+            )
+            mask_row = mask_ref[pl.ds(at, 1), :].astype(jnp.float32)
+            right_made = sigmoid(both[:hidden]) * both[hidden : 2 * hidden] * mask_row
+            left_made = sigmoid(both[2 * hidden : 3 * hidden]) * both[3 * hidden :] * mask_row
+            wide[pl.ds(local + hidden * PITCH, hidden, stride=PITCH), :] = right_made
+            wide[pl.ds(local, hidden, stride=PITCH), :] = left_made
             return carry
 
         lax.fori_loop(0, CHUNK, one_row, 0, unroll=MAKE_UNROLL)
@@ -208,7 +214,7 @@
 
         @pl.when(inner)
         def _():
-            send_edges(right_ends, 0, early, first, CHUNK, send_far, recv_far.at[0, 0], far_q)
+            send_edges(right_ends, 0, early, first, CHUNK, send_far, recv_far.at[0], far_q)
 
         @pl.when((place == 1) & (chunk > 0))
         def _():
@@ -278,13 +284,13 @@
 
     def cross_early(chunk):
         await_part(right_rows(0, early, 0, zone * CHUNK), recv_early.at[chunk])
-        pass_early(edge_q, chunk, far_q, recv_far.at[1, 0])
+        pass_early(edge_q, chunk, far_q, recv_far.at[0])
 
     def cross_near(group):
-        pass_late(hub_q, group, far_q, recv_right.at[0, group], recv_far.at[0, 1 + group])
+        pass_late(hub_q, group, far_q, recv_right.at[0, group], recv_far.at[1 + group])
 
     def cross_edge(group):
-        pass_late(edge_q, group, far_q, recv_right.at[1, group], recv_far.at[1, 1 + group])
+        pass_late(edge_q, group, far_q, recv_right.at[1, group], recv_far.at[1 + group + group // (late - 1)])
 
     def climb_right(group):
         pass_late(edge_q, group, hub_q, recv_right.at[0, group], recv_right.at[1, group])
@@ -359,13 +365,13 @@
         block(chan, count, 2 * half, 2, landed)
 
     def far_block(chan, count, group, landed):
-        for where in range(2):
-            far_part(where, chan, count, group, landed)
+        await_part(right_rows(chan, count, far_first, group_rows * row_count), recv_far.at[group])
+        block(chan, count, 2 * (1 - half), 2, landed)
 
     def far_part(where, chan, count, group, landed):
         from_q = far_q if where == 0 else 3 * (1 - half)
         part = right_rows(chan, count, from_q * zone * row_count, zone * row_count)
-        await_part(part, recv_far.at[where, group])
+        await_part(part, recv_far.at[group])
         block(chan, count, from_q, 1, landed)
 
     def own_triangle():
@@ -504,8 +510,7 @@
         cross_edge(0)
         await_part(left_rows(0, early, hub_q), recv_left.at[0, 0])
         await_part(left_rows(shared, early - shared, edge_q), recv_left.at[1, 0])
-        for where, from_q in ((0, far_q), (1, 3 * (1 - half))):
-            await_part(right_rows(0, early, from_q * zone * row_count, zone * row_count), recv_far.at[where, 0])
+        await_part(right_rows(0, early, far_first, group_rows * row_count), recv_far.at[0])
         pass_on(right_rows(0, shared, far_first, group_rows * row_count), edge_q, recv_down)
         own_triangle()
         block(shared, early - shared, 0, 4, recv_tri.at[0])
@@ -528,7 +533,7 @@
         near_block(share - 1, 1, late, recv_tri.at[1])
         far_part(0, share - 1, 1, late, recv_tri.at[1])
         gather_stats()
-        far_part(1, share - 1, 1, late, recv_tri.at[1])
+        far_part(1, share - 1, 1, late + 1, recv_tri.at[1])
 
     @pl.when(place == 1)
     def _():
@@ -670,7 +675,7 @@
             pltpu.SemaphoreType.DMA,
             pltpu.SemaphoreType.DMA,
             pltpu.SemaphoreType.DMA((2, late)),
-            pltpu.SemaphoreType.DMA((2, 1 + late)),
+            pltpu.SemaphoreType.DMA((2 + late,)),
             pltpu.SemaphoreType.DMA((2,)),
             pltpu.SemaphoreType.DMA,
             pltpu.SemaphoreType.DMA,

time: 104 us -> 104 us (level)
  no operation moved by 1% of the time
where the time goes in v7:
time: 104 us; the launch traced here: 102 us
  Pallas kernels  101 us (97%)
  local copies, waits for them, and re-layouts  1.32 us (1%)
    pallas_call x1, Pallas kernels, fused(): pl.pallas_call(functools.partial(kernel, rows_n, ka_n, EARLY), out_shape=...  101 us

profile of v7, /device:TPU:0, one launch (start us, length us, event | category | flops | bytes accessed | tf_op | source)
XLA Modules:
  0.0 102.2 jit_solution(7614461988790578911)
XLA Ops:
  0.0 100.8 %shard_map.100 = bf16[64,128,128]{2,1,0:T(8,128)(2,1)S(1)} custom-call(bf16[64,128,128]{2,1,0:T(8,128)(2,1)} %pair_hbm.1, s32[64,128]{1,0:T(8,128)} %mask_hbm.1, f32[1,128]{1,0:T(1,128)} %bitcast.4, f32[1,128]{1,0:T(1,128)} %bitcast.5, bf16[128,256]{1,0:T(8,128)(2,1)} %w_proj_hbm.1, bf16[128,256]{1,0:T(8,128)(2,1)} %w_gate_hbm.1, ...), custom_call_target="tpu_custom_call" | custom-call | tf_op jit(solution)/shard_map/pallas_call | solution.py:639
  100.8 1.3 %copy.12 = bf16[64,128,128]{2,1,0:T(8,128)(2,1)} copy(bf16[64,128,128]{2,1,0:T(8,128)(2,1)S(1)} %shard_map.100) | data formatting | bytes 4194304

commit v8 on v7

--- a/solution.py
+++ b/solution.py
@@ -397,7 +397,7 @@
 
         lax.fori_loop(0, chunks, one_chunk, 0)
 
-    for small in smalls[2:]:
+    for small in smalls[2:5]:
         small.wait()
     make_first()
     pl.semaphore_wait(barrier, members - 1 + hubs * (1 - place))
@@ -408,6 +408,8 @@
         send_edges(right_ends, 0, shared, 0, CHUNK, send_right, recv_first.at[0, 0])
 
     send_early_right(0)
+    for small in smalls[5:]:
+        small.wait()
     make_first_left()
     send_early_left(0)
 

time: 104 us -> 104 us (level)
  no operation moved by 1% of the time
where the time goes in v8:
time: 104 us; the launch traced here: 102 us
  Pallas kernels  101 us (97%)
  local copies, waits for them, and re-layouts  1.32 us (1%)
    pallas_call x1, Pallas kernels, fused(): pl.pallas_call(functools.partial(kernel, rows_n, ka_n, EARLY), out_shape=...  101 us

profile of v8, /device:TPU:0, one launch (start us, length us, event | category | flops | bytes accessed | tf_op | source)
XLA Modules:
  0.0 102.1 jit_solution(5982970790592938579)
XLA Ops:
  0.0 100.8 %shard_map.100 = bf16[64,128,128]{2,1,0:T(8,128)(2,1)S(1)} custom-call(bf16[64,128,128]{2,1,0:T(8,128)(2,1)} %pair_hbm.1, s32[64,128]{1,0:T(8,128)} %mask_hbm.1, f32[1,128]{1,0:T(1,128)} %bitcast.4, f32[1,128]{1,0:T(1,128)} %bitcast.5, bf16[128,256]{1,0:T(8,128)(2,1)} %w_proj_hbm.1, bf16[128,256]{1,0:T(8,128)(2,1)} %w_gate_hbm.1, ...), custom_call_target="tpu_custom_call" | custom-call | tf_op jit(solution)/shard_map/pallas_call | solution.py:641
  100.8 1.3 %copy.12 = bf16[64,128,128]{2,1,0:T(8,128)(2,1)} copy(bf16[64,128,128]{2,1,0:T(8,128)(2,1)S(1)} %shard_map.100) | data formatting | bytes 4194304
